TPU v7x, 32 devices: a whole 2x2x4 slice. The times are simulated.
32 devices in a mesh: freq: 4 (over y, core), space: 8 (over z, x).
Axes of the slice: x: 2, y: 2, z: 4, core: 2. Of those that a mesh axis runs over, the one named last changes fastest.
Arguments:
- reflection: float32 [2, 32, 1024, 1024], P(None, 'freq', 'space'), may hold values from -6 to 6
- phase: float32 [32, 1024], P('freq'), may hold values from -3.140625 to 3.140625
- group_index: int32 [32], P('freq'), may hold values from 0 to 3
- widths: int32 [8, 2], P('space'), may hold values from 1 to 128
Outputs:
- corrected: float32 [2, 4, 1024, 1024], P(None, 'freq', None, 'space')
Inputs may be any that keep to these rules, and one draw needn't show every extreme that they name: `group_index`: each frequency belongs to one depth group. `widths`: margins of a patch are at most one column block wide.
All inputs are finite; a program needn't handle non-finite values.
Results may differ from a plain program's by a relative error of at most 0.0003.
Values sent between devices are 32-bit elements; how exact they have to be, the bound alone decides.
No kernel may reach another device: no remote copies, remote signals or barrier semaphores. Data moves between devices by JAX's collectives and lax.ppermute only.
A program may use at most 64 MiB of HBM per device.

v0:
```python
import functools
import math

import jax
import jax.numpy as jnp
import numpy as np
from jax import lax
from jax.experimental import pallas as pl
from jax.experimental.pallas import tpu as pltpu
from jax.sharding import PartitionSpec as P


ITERS = 3
F32 = jnp.float32
BF16 = jnp.bfloat16


def padded(array, sides, width):
    for axis, dim in sides:
        devices, length = (lax.axis_size(axis), array.shape[dim])
        up = [(i, (i + 1) % devices) for i in range(devices)]
        down = [(j, i) for i, j in up]
        last = lax.slice_in_dim(array, length - width, length, axis=dim)
        leading = lax.slice_in_dim(array, 0, width, axis=dim)
        before = lax.ppermute(last, axis, up)
        after = lax.ppermute(leading, axis, down)
        array = jnp.concatenate([before, array, after], axis=dim)
    return array


def factor_tables(length):
    first = 1
    for divisor in range(1, math.isqrt(length) + 1):
        if length % divisor == 0:
            first = divisor
    second = length // first
    scale = 1.0 / math.sqrt(length)
    outer_a = jnp.arange(first, dtype=jnp.int32)
    outer_b = jnp.arange(second, dtype=jnp.int32)
    angle_a = (outer_a[:, None] * outer_a[None, :] % first).astype(jnp.float32) * (
        -2.0 * math.pi / first
    )
    angle_t = (outer_a[:, None] * outer_b[None, :] % length).astype(jnp.float32) * (
        -2.0 * math.pi / length
    )
    angle_b = (outer_b[:, None] * outer_b[None, :] % second).astype(jnp.float32) * (
        -2.0 * math.pi / second
    )
    return (
        jnp.cos(angle_a) * scale,
        jnp.sin(angle_a) * scale,
        jnp.cos(angle_t),
        jnp.sin(angle_t),
        jnp.cos(angle_b),
        jnp.sin(angle_b),
    )


def hmul(left, right):
    return jnp.matmul(
        left, right, precision=lax.Precision.HIGHEST, preferred_element_type=jnp.float32
    )


def heinsum(form, left, right):
    return jnp.einsum(
        form, left, right, precision=lax.Precision.HIGHEST, preferred_element_type=jnp.float32
    )


def complex_mix(form, real_part, imag_part, table_r, table_i):
    out_r = heinsum(form, real_part, table_r) - heinsum(form, imag_part, table_i)
    out_i = heinsum(form, real_part, table_i) + heinsum(form, imag_part, table_r)
    return (out_r, out_i)


def columns_transform(real_part, imag_part, tables):
    first_r, first_i, twist_r, twist_i, second_r, second_i = tables
    shape = real_part.shape
    first = first_r.shape[0]
    second = second_r.shape[0]
    split_r = real_part.reshape(shape[:-1] + (first, second))
    split_i = imag_part.reshape(shape[:-1] + (first, second))
    mid_r, mid_i = complex_mix("...ab,ak->...kb", split_r, split_i, first_r, first_i)
    turn_r = mid_r * twist_r - mid_i * twist_i
    turn_i = mid_r * twist_i + mid_i * twist_r
    out_r, out_i = complex_mix("...kb,bm->...mk", turn_r, turn_i, second_r, second_i)
    return (out_r.reshape(shape), out_i.reshape(shape))


def rows_transform(real_part, imag_part, tables):
    first_r, first_i, twist_r, twist_i, second_r, second_i = tables
    shape = real_part.shape
    first = first_r.shape[0]
    second = second_r.shape[0]
    split_r = real_part.reshape((first, second) + shape[1:])
    split_i = imag_part.reshape((first, second) + shape[1:])
    mid_r, mid_i = complex_mix("abc,ak->kbc", split_r, split_i, first_r, first_i)
    turn_r = mid_r * twist_r[:, :, None] - mid_i * twist_i[:, :, None]
    turn_i = mid_r * twist_i[:, :, None] + mid_i * twist_r[:, :, None]
    out_r, out_i = complex_mix("kbc,bm->mkc", turn_r, turn_i, second_r, second_i)
    return (out_r.reshape(shape), out_i.reshape(shape))


def normalize(real_part, imag_part):
    power = real_part * real_part + imag_part * imag_part
    scale = 1.0 / jnp.sqrt(power + jnp.mean(power) + 1e-06)
    return (real_part * scale, imag_part * scale)


def plain_local(reflection, phase, group_index, widths):
    width = reflection.shape[3]
    count = lax.axis_size("freq")
    spaces = lax.axis_size("space")
    block = width // spaces
    rows_here = reflection.shape[2]
    cosine = jnp.cos(phase)[:, None, :]
    sine = jnp.sin(phase)[:, None, :]
    turned_r = reflection[0] * cosine - reflection[1] * sine
    turned_i = reflection[0] * sine + reflection[1] * cosine
    onehot = (group_index[:, None] == jnp.arange(count, dtype=jnp.int32)[None, :]).astype(
        jnp.float32
    )
    partial_r = jnp.einsum("fg,frn->grn", onehot, turned_r, precision=lax.Precision.HIGHEST)
    partial_i = jnp.einsum("fg,frn->grn", onehot, turned_i, precision=lax.Precision.HIGHEST)
    tables = factor_tables(width)
    summed = lax.psum_scatter(
        jnp.stack([partial_r, partial_i], axis=1), "freq", scatter_dimension=0, tiled=True
    )
    focus_r = summed[0, 0]
    focus_i = summed[0, 1]
    focus_r, focus_i = columns_transform(focus_r, focus_i, tables)
    blocks = jnp.stack([focus_r, focus_i]).reshape(2, rows_here, spaces, block)
    received = lax.all_to_all(blocks, "space", split_axis=2, concat_axis=1, tiled=True)
    piece_r = received[0, :, 0, :]
    piece_i = received[1, :, 0, :]
    out_r, out_i = rows_transform(piece_r, piece_i, tables)
    owned = jnp.stack([out_r, out_i])
    patch = padded(owned, (("space", 2),), block)
    position = jnp.arange(block, dtype=jnp.int32)
    left_keep = (position >= block - widths[0, 0]).astype(jnp.float32)
    right_keep = (position < widths[0, 1]).astype(jnp.float32)
    keep = jnp.concatenate([left_keep, jnp.ones((block,), jnp.float32), right_keep])
    patch_r = patch[0] * keep[None, :]
    patch_i = patch[1] * keep[None, :]
    vector_r, vector_i = normalize(jnp.sum(patch_r, axis=1), jnp.sum(patch_i, axis=1))
    for _ in range(ITERS):
        back_r = hmul(vector_r, patch_r) + hmul(vector_i, patch_i)
        back_i = hmul(vector_i, patch_r) - hmul(vector_r, patch_i)
        next_r = hmul(patch_r, back_r) - hmul(patch_i, back_i)
        next_i = hmul(patch_r, back_i) + hmul(patch_i, back_r)
        vector_r, vector_i = normalize(next_r, next_i)
    own_r = patch[0][:, block : 2 * block]
    own_i = patch[1][:, block : 2 * block]
    fixed_r = vector_r[:, None] * own_r + vector_i[:, None] * own_i
    fixed_i = vector_r[:, None] * own_i - vector_i[:, None] * own_r
    return jnp.stack([fixed_r, fixed_i])[:, None]


def unit_angles(top, n):
    angle = -2.0 * np.pi * (top % n) / n
    return np.cos(angle), np.sin(angle)


def halves(values):
    kind = jnp.dtype(BF16)
    high = values.astype(np.float32).astype(kind)
    low = (values - high.astype(np.float64)).astype(np.float32).astype(kind)
    return jnp.asarray(np.concatenate([high, high, low], axis=1))


def quarter_matrix(width):
    quarter = width // 4
    index = np.arange(quarter)
    real, imag = unit_angles(np.outer(index, index), quarter)
    return real / math.sqrt(width), imag / math.sqrt(width)


def column_tables(width):
    quarter = width // 4
    real, imag = quarter_matrix(width)
    twist = [unit_angles(np.arange(quarter) * k, width) for k in range(4)]
    turn = np.stack([t[0] for t in twist] + [t[1] for t in twist])
    return halves(np.concatenate([real, imag], axis=1)), jnp.asarray(turn, F32)


def row_tables(width, chunk, chunks, block):
    part = block // chunks
    lane = np.arange(2 * block)
    imaginary = lane % block >= part
    row = lane // block * block + chunk * part + lane % part
    real, imag = quarter_matrix(width)
    real, imag = real[:, row], imag[:, row]
    upper = np.where(imaginary, -imag, real)
    lower = np.where(imaginary, real, imag)
    twist = [unit_angles(row * k, width) for k in range(4)]
    sign = np.where(imaginary, 1.0, -1.0)
    turn = np.stack([t[0] for t in twist] + [t[1] * sign for t in twist])
    return halves(np.concatenate([upper, lower], axis=0)), jnp.asarray(turn, F32)


def split(value):
    high = value.astype(BF16)
    return high, (value - high.astype(F32)).astype(BF16)


def cost(micros):
    return pl.CostEstimate(flops=int(micros * 8e7), bytes_accessed=0, transcendentals=0)


def product(table, right):
    high, low = split(right)
    sides = jnp.concatenate([high, low, high], axis=1)
    return lax.dot_general(table, sides, (((1,), (1,)), ((), ())), preferred_element_type=F32)


def turn_kernel(me_ref, group_ref, phase_ref, refl_ref, own_ref, far_ref, send_ref, cos_ref, sin_ref, sum_ref):
    @pl.when(pl.program_id(0) == 0)
    def _():
        cos_ref[...] = jnp.cos(phase_ref[...])
        sin_ref[...] = jnp.sin(phase_ref[...])

    sum_ref[...] = jnp.zeros(sum_ref.shape, F32)
    count = refl_ref.shape[1]
    rows = refl_ref.shape[2]
    for f in range(count):
        slot = group_ref[f] ^ me_ref[0]
        cosine = cos_ref[f : f + 1, :]
        sine = sin_ref[f : f + 1, :]
        for t in range(0, rows, 8):
            real = refl_ref[0, f, t : t + 8, :]
            imag = refl_ref[1, f, t : t + 8, :]
            sum_ref[slot, 0, t : t + 8, :] += real * cosine - imag * sine
            sum_ref[slot, 1, t : t + 8, :] += real * sine + imag * cosine
    own_ref[...] = sum_ref[0]
    far_ref[...] = sum_ref[2]
    send_ref[0] = sum_ref[3]
    send_ref[1] = sum_ref[1]


def turn_sum(me, groups, phase, reflection, first, rows, rows_at):
    _, count, _, width = reflection.shape
    shape = jax.ShapeDtypeStruct((2, rows, width), F32)
    spec = pl.BlockSpec((2, rows_at, width), lambda i: (0, i, 0))
    offset = first // rows_at
    return pl.pallas_call(
        turn_kernel,
        grid=(rows // rows_at,),
        in_specs=[
            pl.BlockSpec(memory_space=pltpu.SMEM),
            pl.BlockSpec(memory_space=pltpu.SMEM),
            pl.BlockSpec((count, width), lambda i: (0, 0)),
            pl.BlockSpec((2, count, rows_at, width), lambda i: (0, 0, i + offset, 0)),
        ],
        out_specs=[spec, spec, pl.BlockSpec((2, 2, rows_at, width), lambda i: (0, 0, i, 0))],
        out_shape=[shape, shape, jax.ShapeDtypeStruct((2, 2, rows, width), F32)],
        scratch_shapes=[pltpu.VMEM((count, width), F32)] * 2 + [pltpu.VMEM((4, 2, rows_at, width), F32)],
        name="turn_sum",
        compiler_params=pltpu.CompilerParams(vmem_limit_bytes=57 * 2**20),
        cost_estimate=cost(4),
    )(me, groups, phase, reflection)


def columns_kernel(place_ref, table_ref, turn_ref, own_ref, core_ref, far_ref, *refs):
    outs = refs[:-1]
    z_ref = refs[-1]
    rows, width = own_ref.shape[1:]
    quarter = width // 4
    block = width // (2 * len(outs))

    def plane(p):
        cuts = [slice(a * quarter, (a + 1) * quarter) for a in range(4)]
        return [own_ref[p, :, c] + core_ref[1, p, :, c] + far_ref[p, :, c] for c in cuts]

    a_r, b_r, c_r, d_r = plane(0)
    a_i, b_i, c_i, d_i = plane(1)
    s0_r, s0_i = a_r + c_r, a_i + c_i
    s1_r, s1_i = a_r - c_r, a_i - c_i
    s2_r, s2_i = b_r + d_r, b_i + d_i
    s3_r, s3_i = b_r - d_r, b_i - d_i
    mixed = (
        (s0_r + s2_r, s0_i + s2_i),
        (s1_r + s3_i, s1_i - s3_r),
        (s0_r - s2_r, s0_i - s2_i),
        (s1_r - s3_i, s1_i + s3_r),
    )
    for pair in range(2):
        stacked = []
        for k in (2 * pair, 2 * pair + 1):
            v_r, v_i = mixed[k]
            if k > 0:
                t_r = turn_ref[k : k + 1, :]
                t_i = turn_ref[4 + k : 5 + k, :]
                v_r, v_i = v_r * t_r - v_i * t_i, v_r * t_i + v_i * t_r
            stacked.append(jnp.concatenate([v_r, -v_i], axis=1))
            stacked.append(jnp.concatenate([v_i, v_r], axis=1))
        out = product(table_ref[...], jnp.concatenate(stacked, axis=0))
        for e in range(2):
            z_ref[pl.ds(2 * pair + e, quarter, stride=4), :] = out[:, 2 * rows * e : 2 * rows * (e + 1)]
    place = place_ref[0]
    for k in range(len(outs)):
        for p in range(2):
            start = pl.multiple_of((place ^ (2 * k + p)) * block, block)
            outs[k][p] = z_ref[pl.ds(start, block), :]


def columns_step(place, tables, own, core, far, spaces):
    _, rows, width = own.shape
    block = width // spaces
    return pl.pallas_call(
        columns_kernel,
        in_specs=[pl.BlockSpec(memory_space=pltpu.SMEM)] + [pl.BlockSpec(memory_space=pltpu.VMEM)] * 5,
        out_specs=[pl.BlockSpec(memory_space=pltpu.VMEM)] * (spaces // 2),
        out_shape=[jax.ShapeDtypeStruct((2, block, 2 * rows), F32)] * (spaces // 2),
        scratch_shapes=[pltpu.VMEM((width, 2 * rows), F32)],
        name="columns_step",
        compiler_params=pltpu.CompilerParams(vmem_limit_bytes=12 * 2**20),
        cost_estimate=cost(3),
    )(place, *tables, own, core, far)


def rows_kernel(sides, origin_ref, table_ref, turn_ref, same_ref, cross_ref, *refs):
    out_ref, pieces_ref = refs[-2:]
    spaces, block, _ = pieces_ref.shape
    quarter = out_ref.shape[1] // 4
    origin = origin_ref[0]
    for k in range(spaces // 2):
        pieces_ref[origin ^ (2 * k)] = same_ref[sides[0], k]
        pieces_ref[origin ^ (2 * k + 1)] = cross_ref[sides[1], k]
    half = block // 2
    lane = lax.broadcasted_iota(jnp.int32, (1, block), 1)
    sign = jnp.where(lane < half, 1.0, -1.0)

    def swap(x):
        return pltpu.roll(x, half, 1)

    def piece(s):
        return pieces_ref[s]

    mixed = [[], [], [], []]
    for e in range(2):
        a, b, c, d = [piece(2 * q + e) for q in range(4)]
        s0, s1, s2 = a + c, a - c, b + d
        s3 = swap(b - d) * sign
        for k, v in enumerate((s0 + s2, s1 + s3, s0 - s2, s1 - s3)):
            if k > 0:
                at = slice(e * block, (e + 1) * block)
                v = v * turn_ref[k : k + 1, at] + swap(v) * turn_ref[4 + k : 5 + k, at]
            mixed[k].append(v)
    for pair in range(2):
        stacked = [jnp.concatenate(mixed[k], axis=1) for k in (2 * pair, 2 * pair + 1)]
        out = product(table_ref[...], jnp.concatenate(stacked, axis=0))
        for e in range(2):
            at = pl.ds(2 * pair + e, quarter, stride=4)
            for p in range(2):
                value = out[p * quarter : (p + 1) * quarter, e * block : (e + 1) * block]
                if len(refs) > 2:
                    value = value + refs[0][p, at, :]
                out_ref[p, at, :] = value


def rows_step(origin, tables, sides, same, cross, *sofar):
    _, pairs, block, _ = same.shape
    width = 2 * pairs * block
    return pl.pallas_call(
        functools.partial(rows_kernel, sides),
        in_specs=[pl.BlockSpec(memory_space=pltpu.SMEM)] + [pl.BlockSpec(memory_space=pltpu.VMEM)] * (4 + len(sofar)),
        out_specs=pl.BlockSpec(memory_space=pltpu.VMEM),
        out_shape=jax.ShapeDtypeStruct((2, width, block), F32),
        scratch_shapes=[pltpu.VMEM((2 * pairs, block, block), F32)],
        name="rows_step",
        compiler_params=pltpu.CompilerParams(vmem_limit_bytes=12 * 2**20),
        cost_estimate=cost(1),
    )(origin, *tables, same, cross, *sofar)


def focus_kernel(place_ref, widths_ref, own_ref, near_in, other_in, out_ref, near_ref, other_ref):
    rows, block = own_ref.shape[1:]
    step = 128
    tiles = rows // step
    position = lax.broadcasted_iota(jnp.int32, (1, block), 1)
    near_left = place_ref[0] % 2
    left = (position >= block - widths_ref[0, 0]).astype(jnp.int32)
    right = (position < widths_ref[0, 1]).astype(jnp.int32)
    near = (left * near_left + right * (1 - near_left)).astype(F32)
    other = (right * near_left + left * (1 - near_left)).astype(F32)

    def masks(t, carry):
        at = pl.ds(pl.multiple_of(t * step, step), step)
        for p in range(2):
            near_ref[p, at, :] = near_in[p, at, :] * near
            other_ref[p, at, :] = other_in[p, at, :] * other
        return carry

    lax.fori_loop(0, tiles, masks, 0)
    blocks = (near_ref, own_ref, other_ref)

    def normal(real, imag, total):
        power = real * real + imag * imag
        scale = lax.rsqrt(power + total / rows + 1e-06)
        return real * scale, imag * scale

    def tile(ref, t):
        return ref[0, t * step : (t + 1) * step, :], ref[1, t * step : (t + 1) * step, :]

    def reduce_rows(parts):
        reals, imags = [], []
        total = jnp.zeros((1, 1), F32)
        for real, imag in parts:
            real = jnp.sum(real, axis=1, keepdims=True)
            imag = jnp.sum(imag, axis=1, keepdims=True)
            total = total + jnp.sum(real * real + imag * imag, axis=0, keepdims=True)
            reals.append(real)
            imags.append(imag)
        return [normal(r, i, total) for r, i in zip(reals, imags)]

    def first():
        for t in range(tiles):
            real = near_ref[0, t * step : (t + 1) * step, :]
            imag = near_ref[1, t * step : (t + 1) * step, :]
            for ref in blocks[1:]:
                r, i = tile(ref, t)
                real, imag = real + r, imag + i
            yield real, imag

    vector = reduce_rows(first())
    for _ in range(ITERS):
        back = []
        for ref in blocks:
            back_r = jnp.zeros((8, block), F32)
            back_i = jnp.zeros((8, block), F32)
            for t in range(tiles):
                r, i = tile(ref, t)
                v_r, v_i = vector[t]
                back_r += jnp.sum((r * v_r + i * v_i).reshape(step // 8, 8, block), axis=0)
                back_i += jnp.sum((r * v_i - i * v_r).reshape(step // 8, 8, block), axis=0)
            back.append((jnp.sum(back_r, axis=0, keepdims=True), jnp.sum(back_i, axis=0, keepdims=True)))

        def forward():
            for t in range(tiles):
                real = imag = None
                for ref, (b_r, b_i) in zip(blocks, back):
                    r, i = tile(ref, t)
                    x, y = r * b_r - i * b_i, r * b_i + i * b_r
                    real, imag = (x, y) if real is None else (real + x, imag + y)
                yield real, imag

        vector = reduce_rows(forward())
    for t in range(tiles):
        r, i = tile(own_ref, t)
        v_r, v_i = vector[t]
        out_ref[0, 0, t * step : (t + 1) * step, :] = v_r * r + v_i * i
        out_ref[1, 0, t * step : (t + 1) * step, :] = v_r * i - v_i * r


def focus_step(place, widths, own, near, other):
    _, rows, block = own.shape
    vmem = pl.BlockSpec(memory_space=pltpu.VMEM)
    return pl.pallas_call(
        focus_kernel,
        in_specs=[pl.BlockSpec(memory_space=pltpu.SMEM)] * 2 + [vmem] * 3,
        out_specs=vmem,
        out_shape=jax.ShapeDtypeStruct((2, 1, rows, block), F32),
        scratch_shapes=[pltpu.VMEM((2, rows, block), F32), pltpu.VMEM((2, rows, block), F32)],
        name="focus_step",
        compiler_params=pltpu.CompilerParams(vmem_limit_bytes=16 * 2**20),
        cost_estimate=cost(6),
    )(place, widths, own, near, other)


CHUNKS = 2


def local(reflection, phase, group_index, widths):
    return focus_all(reflection, phase, group_index, widths)


def focus_all(reflection, phase, group_index, widths):
    rows_here, width = reflection.shape[2:]
    count = lax.axis_size("freq")
    spaces = lax.axis_size("space")
    block = width // spaces
    me = lax.axis_index("freq").astype(jnp.int32)[None]
    place = lax.axis_index("space").astype(jnp.int32)[None]
    near = [(i, i ^ 1) for i in range(count)]
    far = [(i, i ^ 2) for i in range(count)]
    along = [(i, (i + 2 if i % 2 == 0 else i - 2) % spaces) for i in range(spaces)]
    beyond_from = jnp.where(place % 2 == 0, place + (spaces - 2), place + 2) % spaces
    columns = column_tables(width)
    chunk = rows_here // CHUNKS
    sums = [turn_sum(me, group_index, phase, reflection, h * chunk, chunk, 32) for h in range(CHUNKS)]
    cores, fars = [], []
    for h in range(CHUNKS):
        cores.append(lax.ppermute(sums[h][2], "freq", near))
        partial = sums[h][1] + cores[h][0]
        fars.append(lax.ppermute(partial, "freq", far))
    own_block = near_block = other_block = ()
    for h in range(CHUNKS):
        rows = row_tables(width, h, CHUNKS, block)
        pieces = list(columns_step(place, columns, sums[h][0], cores[h], fars[h], spaces))
        for k in range(1, spaces // 2):
            pieces[k] = lax.ppermute(pieces[k], "space", [(i, i ^ (2 * k)) for i in range(spaces)])
        same = jnp.stack(pieces, axis=1)
        cross = lax.ppermute(same, "space", [(i, i ^ 1) for i in range(spaces)])
        beyond = lax.ppermute(jnp.stack([same[1], cross[0]]), "space", along)
        own_block = (rows_step(place, rows, (0, 1), same, cross, *own_block),)
        near_block = (rows_step(place, rows, (1, 0), same, cross, *near_block),)
        other_block = (rows_step(beyond_from, rows, (0, 1), beyond, beyond, *other_block),)
    return focus_step(place, widths, own_block[0], near_block[0], other_block[0])


def solution(mesh):
    in_specs = (P(None, "freq", "space", None), P("freq", None), P("freq"), P("space", None))
    out_specs = P(None, "freq", None, "space")

    def step(reflection, phase, group_index, widths):
        block = reflection.shape[3] // mesh.shape["space"]
        rows = reflection.shape[2] // mesh.shape["space"]
        whole = block % 128 == 0 and rows == 128 and mesh.shape["freq"] == 4 and mesh.shape["space"] == 8
        body = local if whole else plain_local
        return jax.shard_map(
            body, mesh=mesh, in_specs=in_specs, out_specs=out_specs, check_vma=False
        )(reflection, phase, group_index, widths)

    return step
```

profile of v0, /device:TPU:0, one launch (start us, length us, event | category | flops | bytes accessed | tf_op | source)
XLA Modules:
  0.0 88.9 jit_solution(6287263473199814257)
XLA Ops:
  0.0 0.0 copy-start.2
  0.0 0.0 copy-start.9
  0.0 3.9 %turn_sum.3 = (f32[2,64,1024]{2,1,0:T(8,128)}, f32[2,64,1024]{2,1,0:T(8,128)}, f32[2,2,64,1024]{3,2,1,0:T(8,128)}) custom-call(s32[1]{0:T(128)} %bitcast.1.me_ref, s32[8]{0:T(128)} %group_ref.3, f32[8,1024]{1,0:T(8,128)} %phase_ref.3, f32[2,8,128,1024]{3,2,1,0:T(8,128)} %refl_ref.3), custom_call_target="tpu_custom_call" | custom-call | flops 320000000 | tf_op jit(solution)/shard_map/turn_sum/pallas_call | solution.py:246
  3.9 0.0 copy-start.11
  3.9 0.0 copy-start.6
  3.9 0.6 collective-permute-start.6
  4.5 3.8 %turn_sum.2 = (f32[2,64,1024]{2,1,0:T(8,128)}, f32[2,64,1024]{2,1,0:T(8,128)}, f32[2,2,64,1024]{3,2,1,0:T(8,128)}) custom-call(s32[1]{0:T(128)} %bitcast.1.me_ref, s32[8]{0:T(128)} %group_ref.3, f32[8,1024]{1,0:T(8,128)} %phase_ref.3, f32[2,8,128,1024]{3,2,1,0:T(8,128)} %refl_ref.3), custom_call_target="tpu_custom_call" | custom-call | flops 320000000 | tf_op jit(solution)/shard_map/turn_sum/pallas_call | solution.py:246
  8.3 0.0 copy-start.1
  8.3 0.0 copy-start.8
  8.3 0.2 collective-permute-start
  8.5 0.0 collective-permute-done.6.core_ref
  8.5 0.0 copy-start.3
  8.5 0.0 copy-done.11
  8.5 0.9 fusion
  9.3 3.0 %collective-permute-start.7 = (f32[2,64,1024]{2,1,0:T(8,128)}, f32[2,64,1024]{2,1,0:T(8,128)}, u32[]{:S(2)}, u32[]{:S(2)}) collective-permute-start(f32[2,64,1024]{2,1,0:T(8,128)} %fusion), channel_id=1, source_target_pairs={{0,16},{8,24},{16,0},{24,8},{1,17},{9,25},{17,1},{25,9},{2,18},{10... | collective-permute-start | bytes 1572872 | tf_op jit(solution)/shard_map/ppermute | solution.py:496
  12.3 0.0 collective-permute-done.core_ref
  12.3 0.0 copy-done.3
  12.3 1.9 %fusion.1 = f32[2,64,1024]{2,1,0:T(8,128)} fusion(f32[2,64,1024]{2,1,0:T(8,128)} %get-tuple-element.21, f32[2,2,64,1024]{3,2,1,0:T(8,128)S(1)} %collective-permute-done.core_ref), kind=kLoop, calls=%fused_computation.3 | loop fusion | flops 131072 | bytes 1572864 | tf_op jit(solution)/shard_map/add | solution.py:495
  14.2 1.5 %collective-permute-start.1 = (f32[2,64,1024]{2,1,0:T(8,128)}, f32[2,64,1024]{2,1,0:T(8,128)}, u32[]{:S(2)}, u32[]{:S(2)}) collective-permute-start(f32[2,64,1024]{2,1,0:T(8,128)} %fusion.1), channel_id=1, source_target_pairs={{0,16},{8,24},{16,0},{24,8},{1,17},{9,25},{17,1},{25,9},{2,18},{10... | collective-permute-start | bytes 1572872 | tf_op jit(solution)/shard_map/ppermute | solution.py:496
  15.8 9.6 %collective-permute-done.7.far_ref = f32[2,64,1024]{2,1,0:T(8,128)} collective-permute-done((f32[2,64,1024]{2,1,0:T(8,128)}, f32[2,64,1024]{2,1,0:T(8,128)}, u32[]{:S(2)}, u32[]{:S(2)}) %collective-permute-start.7) | collective-permute-done | bytes 524320 | tf_op jit(solution)/shard_map/ppermute | solution.py:496
  25.4 0.0 copy-done.2
  25.4 0.0 copy-done.9
  25.4 0.0 copy-done.6
  25.4 0.0 copy-start.4
  25.4 1.2 %copy-done.4 = f32[2,2,64,1024]{3,2,1,0:T(8,128)S(1)} copy-done((f32[2,2,64,1024]{3,2,1,0:T(8,128)S(1)}, f32[2,2,64,1024]{3,2,1,0:T(8,128)}, u32[]{:S(2)}) %copy-start.4) | copy-done | bytes 1048600
  26.6 0.0 copy-start
  26.6 0.0 copy-start.7
  26.6 1.9 %columns_step.3 = (f32[2,128,128]{2,1,0:T(8,128)S(1)}, f32[2,128,128]{2,1,0:T(8,128)S(1)}, f32[2,128,128]{2,1,0:T(8,128)S(1)}, f32[2,128,128]{2,1,0:T(8,128)S(1)}) custom-call(s32[1]{0:T(128)} %bitcast.place_ref.origin_ref, bf16[256,1536]{1,0:T(8,128)(2,1)S(1)} %copy-done.2, f32[8,256]{1,0:T(8,128)S(1)} %copy-done.9, f32[2,64,1024]{2,1,0:T(8,128)S(1)} %copy-done.6, ...), custom_call_target="tpu_custom_call" | custom-call | flops 240000000 | tf_op jit(solution)/shard_map/columns_step/pallas_call | solution.py:310
  28.5 4.2 %collective-permute-start.10 = (f32[2,128,128]{2,1,0:T(8,128)S(1)}, f32[2,128,128]{2,1,0:T(8,128)S(1)}, u32[]{:S(2)}, u32[]{:S(2)}) collective-permute-start(f32[2,128,128]{2,1,0:T(8,128)S(1)} %get-tuple-element.32), channel_id=1, source_target_pairs={{0,6},{1,7},{2,4},{3,5},{4,2},{5,3},{6,0},{7,1},{8,14},{9,15},{10,... | collective-permute-start | bytes 393224 | tf_op jit(solution)/shard_map/ppermute | solution.py:502
  32.7 0.0 collective-permute-start.9
  32.7 0.6 collective-permute-start.8
  33.3 2.7 %collective-permute-done.1.far_ref = f32[2,64,1024]{2,1,0:T(8,128)} collective-permute-done((f32[2,64,1024]{2,1,0:T(8,128)}, f32[2,64,1024]{2,1,0:T(8,128)}, u32[]{:S(2)}, u32[]{:S(2)}) %collective-permute-start.1) | collective-permute-done | bytes 524320 | tf_op jit(solution)/shard_map/ppermute | solution.py:496
  36.0 1.0 %copy-done.5 = f32[2,64,1024]{2,1,0:T(8,128)S(1)} copy-done((f32[2,64,1024]{2,1,0:T(8,128)S(1)}, f32[2,64,1024]{2,1,0:T(8,128)}, u32[]{:S(2)}) %copy-start.5) | copy-done | bytes 524312
  37.0 1.8 %columns_step.2 = (f32[2,128,128]{2,1,0:T(8,128)S(1)}, f32[2,128,128]{2,1,0:T(8,128)S(1)}, f32[2,128,128]{2,1,0:T(8,128)S(1)}, f32[2,128,128]{2,1,0:T(8,128)S(1)}) custom-call(s32[1]{0:T(128)} %bitcast.place_ref.origin_ref, bf16[256,1536]{1,0:T(8,128)(2,1)S(1)} %copy-done.2, f32[8,256]{1,0:T(8,128)S(1)} %copy-done.9, f32[2,64,1024]{2,1,0:T(8,128)S(1)} %copy-done.5, ...), custom_call_target="tpu_custom_call" | custom-call | flops 240000000 | tf_op jit(solution)/shard_map/columns_step/pallas_call | solution.py:310
  38.8 3.9 %collective-permute-start.4 = (f32[2,128,128]{2,1,0:T(8,128)S(1)}, f32[2,128,128]{2,1,0:T(8,128)S(1)}, u32[]{:S(2)}, u32[]{:S(2)}) collective-permute-start(f32[2,128,128]{2,1,0:T(8,128)S(1)} %get-tuple-element.25), channel_id=1, source_target_pairs={{0,6},{1,7},{2,4},{3,5},{4,2},{5,3},{6,0},{7,1},{8,14},{9,15},{10,... | collective-permute-start | bytes 393224 | tf_op jit(solution)/shard_map/ppermute | solution.py:502
  42.7 0.0 collective-permute-start.3
  42.7 0.0 collective-permute-done.10
  42.7 0.6 collective-permute-start.2
  43.4 0.0 collective-permute-done.9
  43.4 0.0 collective-permute-done.8
  43.4 1.7 %collective-permute-start.11 = (f32[2,4,128,128]{3,2,1,0:T(8,128)S(1)}, f32[2,4,128,128]{3,2,1,0:T(8,128)S(1)}, u32[]{:S(2)}, u32[]{:S(2)}) collective-permute-start(f32[2,4,128,128]{3,2,1,0:T(8,128)S(1)} %pad_maximum_fusion.1.same_ref), channel_id=1, source_target_pairs={{0,1},{1,0},{2,3},{3,2},{4,5},{5,4},{6,7},{7,6},{8,9},{9,8},{10,11... | collective-permute-start | bytes 1572872 | tf_op jit(solution)/shard_map/ppermute | solution.py:504
  45.1 2.0 %collective-permute-done.4 = f32[2,128,128]{2,1,0:T(8,128)S(1)} collective-permute-done((f32[2,128,128]{2,1,0:T(8,128)S(1)}, f32[2,128,128]{2,1,0:T(8,128)S(1)}, u32[]{:S(2)}, u32[]{:S(2)}) %collective-permute-start.4) | collective-permute-done | bytes 131104 | tf_op jit(solution)/shard_map/ppermute | solution.py:502
  47.1 6.4 %collective-permute-done.3 = f32[2,128,128]{2,1,0:T(8,128)S(1)} collective-permute-done((f32[2,128,128]{2,1,0:T(8,128)S(1)}, f32[2,128,128]{2,1,0:T(8,128)S(1)}, u32[]{:S(2)}, u32[]{:S(2)}) %collective-permute-start.3) | collective-permute-done | bytes 131104 | tf_op jit(solution)/shard_map/ppermute | solution.py:502
  53.4 0.0 collective-permute-done.2
  53.5 1.5 %collective-permute-start.5 = (f32[2,4,128,128]{3,2,1,0:T(8,128)S(1)}, f32[2,4,128,128]{3,2,1,0:T(8,128)S(1)}, u32[]{:S(2)}, u32[]{:S(2)}) collective-permute-start(f32[2,4,128,128]{3,2,1,0:T(8,128)S(1)} %pad_maximum_fusion.same_ref), channel_id=1, source_target_pairs={{0,1},{1,0},{2,3},{3,2},{4,5},{5,4},{6,7},{7,6},{8,9},{9,8},{10,11... | collective-permute-start | bytes 1572872 | tf_op jit(solution)/shard_map/ppermute | solution.py:504
  55.1 1.2 %collective-permute-done.11.cross_ref = f32[2,4,128,128]{3,2,1,0:T(8,128)S(1)} collective-permute-done((f32[2,4,128,128]{3,2,1,0:T(8,128)S(1)}, f32[2,4,128,128]{3,2,1,0:T(8,128)S(1)}, u32[]{:S(2)}, u32[]{:S(2)}) %collective-permute-start.11) | collective-permute-done | bytes 524320 | tf_op jit(solution)/shard_map/ppermute | solution.py:504
  56.3 3.4 %collective-permute-start.13 = (f32[2,4,128,128]{3,2,1,0:T(8,128)S(1)}, f32[2,4,128,128]{3,2,1,0:T(8,128)S(1)}, u32[]{:S(2)}, u32[]{:S(2)}) collective-permute-start(f32[2,4,128,128]{3,2,1,0:T(8,128)S(1)} %pad_maximum_fusion.3), channel_id=1, source_target_pairs={{0,2},{1,7},{2,4},{3,1},{4,6},{5,3},{6,0},{7,5},{8,10},{9,15},{10,... | collective-permute-start | bytes 1572872 | tf_op jit(solution)/shard_map/ppermute | solution.py:505
  59.8 7.4 %collective-permute-done.5.cross_ref = f32[2,4,128,128]{3,2,1,0:T(8,128)S(1)} collective-permute-done((f32[2,4,128,128]{3,2,1,0:T(8,128)S(1)}, f32[2,4,128,128]{3,2,1,0:T(8,128)S(1)}, u32[]{:S(2)}, u32[]{:S(2)}) %collective-permute-start.5) | collective-permute-done | bytes 524320 | tf_op jit(solution)/shard_map/ppermute | solution.py:504
  67.2 1.6 %collective-permute-start.12 = (f32[2,4,128,128]{3,2,1,0:T(8,128)S(1)}, f32[2,4,128,128]{3,2,1,0:T(8,128)S(1)}, u32[]{:S(2)}, u32[]{:S(2)}) collective-permute-start(f32[2,4,128,128]{3,2,1,0:T(8,128)S(1)} %pad_maximum_fusion.2), channel_id=1, source_target_pairs={{0,2},{1,7},{2,4},{3,1},{4,6},{5,3},{6,0},{7,5},{8,10},{9,15},{10,... | collective-permute-start | bytes 1572872 | tf_op jit(solution)/shard_map/ppermute | solution.py:505
  68.8 0.0 copy-done.1
  68.8 0.0 copy-done.8
  68.9 0.8 rows_step.6.refs_0_
  69.6 0.0 copy-start.10
  69.7 0.8 rows_step.8.refs_0_
  70.5 0.0 copy-done
  70.5 0.0 copy-done.7
  70.5 0.8 rows_step.7.own_ref
  71.3 0.8 rows_step.9.near_in
  72.1 0.0 collective-permute-done.13.same_ref.cross_ref
  72.1 0.8 rows_step.10.refs_0_
  72.9 9.1 %collective-permute-done.12.same_ref.cross_ref = f32[2,4,128,128]{3,2,1,0:T(8,128)S(1)} collective-permute-done((f32[2,4,128,128]{3,2,1,0:T(8,128)S(1)}, f32[2,4,128,128]{3,2,1,0:T(8,128)S(1)}, u32[]{:S(2)}, u32[]{:S(2)}) %collective-permute-start.12) | collective-permute-done | bytes 524320 | tf_op jit(solution)/shard_map/ppermute | solution.py:505
  82.0 0.8 rows_step.11.other_in
  82.8 0.0 copy-done.10
  82.8 6.1 %focus_step.1 = f32[2,1,1024,128]{3,2,1,0:T(8,128)} custom-call(s32[1]{0:T(128)} %bitcast.place_ref.origin_ref, s32[1,2]{1,0:T(1,128)S(1)} %copy-done.10, f32[2,1024,128]{2,1,0:T(8,128)S(1)} %rows_step.7.own_ref, f32[2,1024,128]{2,1,0:T(8,128)S(1)} %rows_step.9.near_in, f32[2,1024,128]{2,1,0:T(8,128)S(1)} %rows_step.11.other_in), custom_call_target="tpu_custom_call" | custom-call | flops 480000000 | tf_op jit(solution)/shard_map/focus_step/pallas_call | solution.py:459
  (9 shorter events, 0.2 us)
Async XLA Ops:
  0.0 25.4 %copy-start.2 = (bf16[256,1536]{1,0:T(8,128)(2,1)S(1)}, bf16[256,1536]{1,0:T(8,128)(2,1)}, u32[]{:S(2)}) copy-start(bf16[256,1536]{1,0:T(8,128)(2,1)} %constant.58.clone.table_ref) | copy-start | bytes 2359300
  0.0 25.4 %copy-start.9 = (f32[8,256]{1,0:T(8,128)S(1)}, f32[8,256]{1,0:T(8,128)}, u32[]{:S(2)}) copy-start(f32[8,256]{1,0:T(8,128)} %constant.59.clone.turn_ref) | copy-start | bytes 24580
  3.9 4.6 %copy-start.11 = (f32[2,64,1024]{2,1,0:T(8,128)S(1)}, f32[2,64,1024]{2,1,0:T(8,128)}, u32[]{:S(2)}) copy-start(f32[2,64,1024]{2,1,0:T(8,128)} %get-tuple-element.28) | copy-start | bytes 1572868
  3.9 21.5 %copy-start.6 = (f32[2,64,1024]{2,1,0:T(8,128)S(1)}, f32[2,64,1024]{2,1,0:T(8,128)}, u32[]{:S(2)}) copy-start(f32[2,64,1024]{2,1,0:T(8,128)} %get-tuple-element.26.own_ref) | copy-start | bytes 1572868
  3.9 4.5 %collective-permute-start.6 = (f32[2,2,64,1024]{3,2,1,0:T(8,128)}, f32[2,2,64,1024]{3,2,1,0:T(8,128)S(1)}, u32[]{:S(2)}, u32[]{:S(2)}) collective-permute-start(f32[2,2,64,1024]{3,2,1,0:T(8,128)} %get-tuple-element.27), channel_id=1, source_target_pairs={{0,8},{8,0},{16,24},{24,16},{1,9},{9,1},{17,25},{25,17},{2,10},{10... | collective-permute-start | bytes 3145736 | tf_op jit(solution)/shard_map/ppermute | solution.py:494
  8.3 60.6 %copy-start.1 = (bf16[512,768]{1,0:T(8,128)(2,1)S(1)}, bf16[512,768]{1,0:T(8,128)(2,1)}, u32[]{:S(2)}) copy-start(bf16[512,768]{1,0:T(8,128)(2,1)} %constant.60.clone.table_ref) | copy-start | bytes 2359300
  8.3 60.6 %copy-start.8 = (f32[8,256]{1,0:T(8,128)S(1)}, f32[8,256]{1,0:T(8,128)}, u32[]{:S(2)}) copy-start(f32[8,256]{1,0:T(8,128)} %constant.61.clone.turn_ref) | copy-start | bytes 24580
  8.3 4.0 %collective-permute-start = (f32[2,2,64,1024]{3,2,1,0:T(8,128)}, f32[2,2,64,1024]{3,2,1,0:T(8,128)S(1)}, u32[]{:S(2)}, u32[]{:S(2)}) collective-permute-start(f32[2,2,64,1024]{3,2,1,0:T(8,128)} %get-tuple-element.20), channel_id=1, source_target_pairs={{0,8},{8,0},{16,24},{24,16},{1,9},{9,1},{17,25},{25,17},{2,10},{10... | collective-permute-start | bytes 3145736 | tf_op jit(solution)/shard_map/ppermute | solution.py:494
  8.5 3.9 %copy-start.3 = (f32[2,2,64,1024]{3,2,1,0:T(8,128)}, f32[2,2,64,1024]{3,2,1,0:T(8,128)S(1)}, u32[]{:S(2)}) copy-start(f32[2,2,64,1024]{3,2,1,0:T(8,128)S(1)} %collective-permute-done.6.core_ref) | copy-start | bytes 3145732
  9.3 16.1 %collective-permute-start.7 = (f32[2,64,1024]{2,1,0:T(8,128)}, f32[2,64,1024]{2,1,0:T(8,128)}, u32[]{:S(2)}, u32[]{:S(2)}) collective-permute-start(f32[2,64,1024]{2,1,0:T(8,128)} %fusion), channel_id=1, source_target_pairs={{0,16},{8,24},{16,0},{24,8},{1,17},{9,25},{17,1},{25,9},{2,18},{10... | collective-permute-start | bytes 1572872 | tf_op jit(solution)/shard_map/ppermute | solution.py:496
  14.2 21.8 %collective-permute-start.1 = (f32[2,64,1024]{2,1,0:T(8,128)}, f32[2,64,1024]{2,1,0:T(8,128)}, u32[]{:S(2)}, u32[]{:S(2)}) collective-permute-start(f32[2,64,1024]{2,1,0:T(8,128)} %fusion.1), channel_id=1, source_target_pairs={{0,16},{8,24},{16,0},{24,8},{1,17},{9,25},{17,1},{25,9},{2,18},{10... | collective-permute-start | bytes 1572872 | tf_op jit(solution)/shard_map/ppermute | solution.py:496
  25.4 1.2 %copy-start.4 = (f32[2,2,64,1024]{3,2,1,0:T(8,128)S(1)}, f32[2,2,64,1024]{3,2,1,0:T(8,128)}, u32[]{:S(2)}) copy-start(f32[2,2,64,1024]{3,2,1,0:T(8,128)} %copy-done.3) | copy-start | bytes 3145732
  26.6 43.8 %copy-start = (bf16[512,768]{1,0:T(8,128)(2,1)S(1)}, bf16[512,768]{1,0:T(8,128)(2,1)}, u32[]{:S(2)}) copy-start(bf16[512,768]{1,0:T(8,128)(2,1)} %constant.62.clone.table_ref) | copy-start | bytes 2359300
  26.6 43.8 %copy-start.7 = (f32[8,256]{1,0:T(8,128)S(1)}, f32[8,256]{1,0:T(8,128)}, u32[]{:S(2)}) copy-start(f32[8,256]{1,0:T(8,128)} %constant.63.clone.turn_ref) | copy-start | bytes 24580
  28.5 14.2 %collective-permute-start.10 = (f32[2,128,128]{2,1,0:T(8,128)S(1)}, f32[2,128,128]{2,1,0:T(8,128)S(1)}, u32[]{:S(2)}, u32[]{:S(2)}) collective-permute-start(f32[2,128,128]{2,1,0:T(8,128)S(1)} %get-tuple-element.32), channel_id=1, source_target_pairs={{0,6},{1,7},{2,4},{3,5},{4,2},{5,3},{6,0},{7,1},{8,14},{9,15},{10,... | collective-permute-start | bytes 393224 | tf_op jit(solution)/shard_map/ppermute | solution.py:502
  32.7 10.7 %collective-permute-start.9 = (f32[2,128,128]{2,1,0:T(8,128)S(1)}, f32[2,128,128]{2,1,0:T(8,128)S(1)}, u32[]{:S(2)}, u32[]{:S(2)}) collective-permute-start(f32[2,128,128]{2,1,0:T(8,128)S(1)} %get-tuple-element.31), channel_id=1, source_target_pairs={{0,4},{1,5},{2,6},{3,7},{4,0},{5,1},{6,2},{7,3},{8,12},{9,13},{10,... | collective-permute-start | bytes 393224 | tf_op jit(solution)/shard_map/ppermute | solution.py:502
  32.7 10.7 %collective-permute-start.8 = (f32[2,128,128]{2,1,0:T(8,128)S(1)}, f32[2,128,128]{2,1,0:T(8,128)S(1)}, u32[]{:S(2)}, u32[]{:S(2)}) collective-permute-start(f32[2,128,128]{2,1,0:T(8,128)S(1)} %get-tuple-element.30), channel_id=1, source_target_pairs={{0,2},{1,3},{2,0},{3,1},{4,6},{5,7},{6,4},{7,5},{8,10},{9,11},{10,... | collective-permute-start | bytes 393224 | tf_op jit(solution)/shard_map/ppermute | solution.py:502
  36.0 1.0 %copy-start.5 = (f32[2,64,1024]{2,1,0:T(8,128)S(1)}, f32[2,64,1024]{2,1,0:T(8,128)}, u32[]{:S(2)}) copy-start(f32[2,64,1024]{2,1,0:T(8,128)} %get-tuple-element.19.own_ref) | copy-start | bytes 1572868
  38.8 8.3 %collective-permute-start.4 = (f32[2,128,128]{2,1,0:T(8,128)S(1)}, f32[2,128,128]{2,1,0:T(8,128)S(1)}, u32[]{:S(2)}, u32[]{:S(2)}) collective-permute-start(f32[2,128,128]{2,1,0:T(8,128)S(1)} %get-tuple-element.25), channel_id=1, source_target_pairs={{0,6},{1,7},{2,4},{3,5},{4,2},{5,3},{6,0},{7,1},{8,14},{9,15},{10,... | collective-permute-start | bytes 393224 | tf_op jit(solution)/shard_map/ppermute | solution.py:502
  42.7 10.7 %collective-permute-start.3 = (f32[2,128,128]{2,1,0:T(8,128)S(1)}, f32[2,128,128]{2,1,0:T(8,128)S(1)}, u32[]{:S(2)}, u32[]{:S(2)}) collective-permute-start(f32[2,128,128]{2,1,0:T(8,128)S(1)} %get-tuple-element.24), channel_id=1, source_target_pairs={{0,4},{1,5},{2,6},{3,7},{4,0},{5,1},{6,2},{7,3},{8,12},{9,13},{10,... | collective-permute-start | bytes 393224 | tf_op jit(solution)/shard_map/ppermute | solution.py:502
  42.7 10.7 %collective-permute-start.2 = (f32[2,128,128]{2,1,0:T(8,128)S(1)}, f32[2,128,128]{2,1,0:T(8,128)S(1)}, u32[]{:S(2)}, u32[]{:S(2)}) collective-permute-start(f32[2,128,128]{2,1,0:T(8,128)S(1)} %get-tuple-element.23), channel_id=1, source_target_pairs={{0,2},{1,3},{2,0},{3,1},{4,6},{5,7},{6,4},{7,5},{8,10},{9,11},{10,... | collective-permute-start | bytes 393224 | tf_op jit(solution)/shard_map/ppermute | solution.py:502
  43.4 12.9 %collective-permute-start.11 = (f32[2,4,128,128]{3,2,1,0:T(8,128)S(1)}, f32[2,4,128,128]{3,2,1,0:T(8,128)S(1)}, u32[]{:S(2)}, u32[]{:S(2)}) collective-permute-start(f32[2,4,128,128]{3,2,1,0:T(8,128)S(1)} %pad_maximum_fusion.1.same_ref), channel_id=1, source_target_pairs={{0,1},{1,0},{2,3},{3,2},{4,5},{5,4},{6,7},{7,6},{8,9},{9,8},{10,11... | collective-permute-start | bytes 1572872 | tf_op jit(solution)/shard_map/ppermute | solution.py:504
  53.5 13.7 %collective-permute-start.5 = (f32[2,4,128,128]{3,2,1,0:T(8,128)S(1)}, f32[2,4,128,128]{3,2,1,0:T(8,128)S(1)}, u32[]{:S(2)}, u32[]{:S(2)}) collective-permute-start(f32[2,4,128,128]{3,2,1,0:T(8,128)S(1)} %pad_maximum_fusion.same_ref), channel_id=1, source_target_pairs={{0,1},{1,0},{2,3},{3,2},{4,5},{5,4},{6,7},{7,6},{8,9},{9,8},{10,11... | collective-permute-start | bytes 1572872 | tf_op jit(solution)/shard_map/ppermute | solution.py:504
  56.3 15.8 %collective-permute-start.13 = (f32[2,4,128,128]{3,2,1,0:T(8,128)S(1)}, f32[2,4,128,128]{3,2,1,0:T(8,128)S(1)}, u32[]{:S(2)}, u32[]{:S(2)}) collective-permute-start(f32[2,4,128,128]{3,2,1,0:T(8,128)S(1)} %pad_maximum_fusion.3), channel_id=1, source_target_pairs={{0,2},{1,7},{2,4},{3,1},{4,6},{5,3},{6,0},{7,5},{8,10},{9,15},{10,... | collective-permute-start | bytes 1572872 | tf_op jit(solution)/shard_map/ppermute | solution.py:505
  67.2 14.8 %collective-permute-start.12 = (f32[2,4,128,128]{3,2,1,0:T(8,128)S(1)}, f32[2,4,128,128]{3,2,1,0:T(8,128)S(1)}, u32[]{:S(2)}, u32[]{:S(2)}) collective-permute-start(f32[2,4,128,128]{3,2,1,0:T(8,128)S(1)} %pad_maximum_fusion.2), channel_id=1, source_target_pairs={{0,2},{1,7},{2,4},{3,1},{4,6},{5,3},{6,0},{7,5},{8,10},{9,15},{10,... | collective-permute-start | bytes 1572872 | tf_op jit(solution)/shard_map/ppermute | solution.py:505
  69.6 13.2 %copy-start.10 = (s32[1,2]{1,0:T(1,128)S(1)}, s32[1,2]{1,0:T(1,128)}, u32[]{:S(2)}) copy-start(s32[1,2]{1,0:T(1,128)} %widths_ref.1) | copy-start | bytes 28
where the time goes:
time: 89.2 us; the launch traced here: 88.9 us
  waiting for transfers between devices  38.4 us (43%)
  starting transfers between devices  22.9 us (26%)
  Pallas kernels  22.2 us (25%)
  other arithmetic  2.92 us (3%)
  local copies, waits for them, and re-layouts  2.37 us (3%)
    ppermute x2, waiting for transfers between devices, focus_all(): fars.append(lax.ppermute(partial, 'freq', far))  12.3 us
    ppermute x6, starting transfers between devices, focus_all(): lax.ppermute(pieces[k], 'space', [(i, i ^ 2 * k) for i in range(spaces)])  9.34 us
    ppermute x2, waiting for transfers between devices, focus_all(): beyond = lax.ppermute(jnp.stack([same[1], cross[0]]), 'space', along)  9.12 us
    ppermute x2, waiting for transfers between devices, focus_all(): cross = lax.ppermute(same, 'space', [(i, i ^ 1) for i in range(spaces)])  8.58 us
    ppermute x6, waiting for transfers between devices, focus_all(): lax.ppermute(pieces[k], 'space', [(i, i ^ 2 * k) for i in range(spaces)])  8.34 us
    pallas_call x2, Pallas kernels, turn_sum(): pl.pallas_call(turn_kernel, grid=(rows // rows_at,), in_specs=[pl.BlockSp...  7.72 us
    pallas_call x1, Pallas kernels, focus_step(): pl.pallas_call(focus_kernel, in_specs=[pl.BlockSpec(memory_space=pltpu.SM...  6.07 us
    ppermute x2, starting transfers between devices, focus_all(): beyond = lax.ppermute(jnp.stack([same[1], cross[0]]), 'space', along)  5.06 us
  transfers between devices with their start and end apart: 14, of which 7 were waited for; matrix products, arithmetic and copies ran while one was open for 3% of the time, Pallas kernels for 13%

commit v1 on v0

--- a/solution.py
+++ b/solution.py
@@ -1,4 +1,3 @@
-import functools
 import math
 
 import jax
@@ -230,8 +229,10 @@
         for t in range(0, rows, 8):
             real = refl_ref[0, f, t : t + 8, :]
             imag = refl_ref[1, f, t : t + 8, :]
-            sum_ref[slot, 0, t : t + 8, :] += real * cosine - imag * sine
-            sum_ref[slot, 1, t : t + 8, :] += real * sine + imag * cosine
+            sum_r = sum_ref[slot, 0, t : t + 8, :]
+            sum_i = sum_ref[slot, 1, t : t + 8, :]
+            sum_ref[slot, 0, t : t + 8, :] = sum_r + (real * cosine - imag * sine)
+            sum_ref[slot, 1, t : t + 8, :] = sum_i + (real * sine + imag * cosine)
     own_ref[...] = sum_ref[0]
     far_ref[...] = sum_ref[2]
     send_ref[0] = sum_ref[3]
@@ -256,12 +257,12 @@
         out_shape=[shape, shape, jax.ShapeDtypeStruct((2, 2, rows, width), F32)],
         scratch_shapes=[pltpu.VMEM((count, width), F32)] * 2 + [pltpu.VMEM((4, 2, rows_at, width), F32)],
         name="turn_sum",
-        compiler_params=pltpu.CompilerParams(vmem_limit_bytes=57 * 2**20),
+        compiler_params=pltpu.CompilerParams(vmem_limit_bytes=56 * 2**20),
         cost_estimate=cost(4),
     )(me, groups, phase, reflection)
 
 
-def columns_kernel(place_ref, table_ref, turn_ref, own_ref, core_ref, far_ref, *refs):
+def columns_kernel(place_ref, table_ref, turn_ref, own_ref, far_ref, *refs):
     outs = refs[:-1]
     z_ref = refs[-1]
     rows, width = own_ref.shape[1:]
@@ -270,7 +271,7 @@
 
     def plane(p):
         cuts = [slice(a * quarter, (a + 1) * quarter) for a in range(4)]
-        return [own_ref[p, :, c] + core_ref[1, p, :, c] + far_ref[p, :, c] for c in cuts]
+        return [own_ref[p, :, c] + far_ref[p, :, c] for c in cuts]
 
     a_r, b_r, c_r, d_r = plane(0)
     a_i, b_i, c_i, d_i = plane(1)
@@ -304,29 +305,29 @@
             outs[k][p] = z_ref[pl.ds(start, block), :]
 
 
-def columns_step(place, tables, own, core, far, spaces):
+def columns_step(place, tables, own, far, spaces):
     _, rows, width = own.shape
     block = width // spaces
     return pl.pallas_call(
         columns_kernel,
-        in_specs=[pl.BlockSpec(memory_space=pltpu.SMEM)] + [pl.BlockSpec(memory_space=pltpu.VMEM)] * 5,
+        in_specs=[pl.BlockSpec(memory_space=pltpu.SMEM)] + [pl.BlockSpec(memory_space=pltpu.VMEM)] * 4,
         out_specs=[pl.BlockSpec(memory_space=pltpu.VMEM)] * (spaces // 2),
         out_shape=[jax.ShapeDtypeStruct((2, block, 2 * rows), F32)] * (spaces // 2),
         scratch_shapes=[pltpu.VMEM((width, 2 * rows), F32)],
         name="columns_step",
         compiler_params=pltpu.CompilerParams(vmem_limit_bytes=12 * 2**20),
         cost_estimate=cost(3),
-    )(place, *tables, own, core, far)
-
-
-def rows_kernel(sides, origin_ref, table_ref, turn_ref, same_ref, cross_ref, *refs):
+    )(place, *tables, own, far)
+
+
+def rows_kernel(origin_ref, table_ref, turn_ref, same_ref, cross_ref, *refs):
     out_ref, pieces_ref = refs[-2:]
     spaces, block, _ = pieces_ref.shape
     quarter = out_ref.shape[1] // 4
     origin = origin_ref[0]
     for k in range(spaces // 2):
-        pieces_ref[origin ^ (2 * k)] = same_ref[sides[0], k]
-        pieces_ref[origin ^ (2 * k + 1)] = cross_ref[sides[1], k]
+        pieces_ref[origin ^ (2 * k)] = same_ref[k]
+        pieces_ref[origin ^ (2 * k + 1)] = cross_ref[k]
     half = block // 2
     lane = lax.broadcasted_iota(jnp.int32, (1, block), 1)
     sign = jnp.where(lane < half, 1.0, -1.0)
@@ -359,11 +360,11 @@
                 out_ref[p, at, :] = value
 
 
-def rows_step(origin, tables, sides, same, cross, *sofar):
-    _, pairs, block, _ = same.shape
+def rows_step(origin, tables, same, cross, *sofar):
+    pairs, block, _ = same.shape
     width = 2 * pairs * block
     return pl.pallas_call(
-        functools.partial(rows_kernel, sides),
+        rows_kernel,
         in_specs=[pl.BlockSpec(memory_space=pltpu.SMEM)] + [pl.BlockSpec(memory_space=pltpu.VMEM)] * (4 + len(sofar)),
         out_specs=pl.BlockSpec(memory_space=pltpu.VMEM),
         out_shape=jax.ShapeDtypeStruct((2, width, block), F32),
@@ -488,24 +489,28 @@
     beyond_from = jnp.where(place % 2 == 0, place + (spaces - 2), place + 2) % spaces
     columns = column_tables(width)
     chunk = rows_here // CHUNKS
-    sums = [turn_sum(me, group_index, phase, reflection, h * chunk, chunk, 32) for h in range(CHUNKS)]
-    cores, fars = [], []
+    cores, fars, mine = [], [], []
+    sums = []
     for h in range(CHUNKS):
+        sums.append(turn_sum(me, group_index, phase, reflection, h * chunk, chunk, 32))
         cores.append(lax.ppermute(sums[h][2], "freq", near))
         partial = sums[h][1] + cores[h][0]
+        mine.append(sums[h][0] + cores[h][1])
         fars.append(lax.ppermute(partial, "freq", far))
     own_block = near_block = other_block = ()
     for h in range(CHUNKS):
         rows = row_tables(width, h, CHUNKS, block)
-        pieces = list(columns_step(place, columns, sums[h][0], cores[h], fars[h], spaces))
+        pieces = list(columns_step(place, columns, mine[h], fars[h], spaces))
         for k in range(1, spaces // 2):
             pieces[k] = lax.ppermute(pieces[k], "space", [(i, i ^ (2 * k)) for i in range(spaces)])
-        same = jnp.stack(pieces, axis=1)
-        cross = lax.ppermute(same, "space", [(i, i ^ 1) for i in range(spaces)])
-        beyond = lax.ppermute(jnp.stack([same[1], cross[0]]), "space", along)
-        own_block = (rows_step(place, rows, (0, 1), same, cross, *own_block),)
-        near_block = (rows_step(place, rows, (1, 0), same, cross, *near_block),)
-        other_block = (rows_step(beyond_from, rows, (0, 1), beyond, beyond, *other_block),)
+        own_same, near_same = [jnp.stack([piece[p] for piece in pieces]) for p in range(2)]
+        across = [(i, i ^ 1) for i in range(spaces)]
+        near_cross = lax.ppermute(own_same, "space", across)
+        own_cross = lax.ppermute(near_same, "space", across)
+        beyond = lax.ppermute(jnp.stack([near_same, near_cross]), "space", along)
+        own_block = (rows_step(place, rows, own_same, own_cross, *own_block),)
+        near_block = (rows_step(place, rows, near_same, near_cross, *near_block),)
+        other_block = (rows_step(beyond_from, rows, beyond[0], beyond[1], *other_block),)
     return focus_step(place, widths, own_block[0], near_block[0], other_block[0])
 
 

time: 89.2 us -> 95.9 us (1.075)
  waiting for transfers between devices: 38.4 us -> 45.7 us
  local copies, waits for them, and re-layouts: 2.37 us -> 0.19 us
  starting transfers between devices: 22.9 us -> 24.2 us
    ppermute x4 -> x6, waiting for transfers between devices: 17.7 us -> 23.9 us  [the longest x2 10.9 us: focus_all(): near_cross = lax.ppermute(own_same, 'space', across)]
    ppermute x6, starting transfers between devices: 9.34 us -> 13.5 us  [focus_all(): lax.ppermute(pieces[k], 'space', [(i, i ^ 2 * k) for i in range(spaces)])]
    ppermute x4 -> x6, starting transfers between devices: 8.3 us -> 5.57 us  [the longest x2 2.16 us: focus_all(): near_cross = lax.ppermute(own_same, 'space', across)]
    unnamed x24 -> x18, local copies, waits for them, and re-layouts: 2.3 us -> 0.05 us
    ppermute x2, waiting for transfers between devices: 12.3 us -> 13.5 us  [focus_all(): fars.append(lax.ppermute(partial, 'freq', far))]
  transfers between devices with their start and end apart: 14 -> 16, of which waited for: 7 -> 11; matrix products, arithmetic and copies ran while one was open for 3% -> 3% of each run, Pallas kernels for 13% -> 12%
where the time goes in v1:
time: 95.9 us; the launch traced here: 95.7 us
  waiting for transfers between devices  45.7 us (48%)
  starting transfers between devices  24.2 us (25%)
  Pallas kernels  22.1 us (23%)
  other arithmetic  3.23 us (3%)
    ppermute x2, waiting for transfers between devices, focus_all(): fars.append(lax.ppermute(partial, 'freq', far))  13.5 us
    ppermute x6, starting transfers between devices, focus_all(): lax.ppermute(pieces[k], 'space', [(i, i ^ 2 * k) for i in range(spaces)])  13.5 us
    ppermute x2, waiting for transfers between devices, focus_all(): near_cross = lax.ppermute(own_same, 'space', across)  10.9 us
    ppermute x6, waiting for transfers between devices, focus_all(): lax.ppermute(pieces[k], 'space', [(i, i ^ 2 * k) for i in range(spaces)])  8.31 us
    pallas_call x2, Pallas kernels, turn_sum(): pl.pallas_call(turn_kernel, grid=(rows // rows_at,), in_specs=[pl.BlockSp...  7.69 us
    ppermute x2, waiting for transfers between devices, focus_all(): beyond = lax.ppermute(jnp.stack([near_same, near_cross]), 'space', along)  7.31 us
    pallas_call x1, Pallas kernels, focus_step(): pl.pallas_call(focus_kernel, in_specs=[pl.BlockSpec(memory_space=pltpu.SM...  6.14 us
    ppermute x2, waiting for transfers between devices, focus_all(): own_cross = lax.ppermute(near_same, 'space', across)  5.7 us
  transfers between devices with their start and end apart: 16, of which 11 were waited for; matrix products, arithmetic and copies ran while one was open for 3% of the time, Pallas kernels for 12%

profile of v1, /device:TPU:0, one launch (start us, length us, event | category | flops | bytes accessed | tf_op | source)
XLA Modules:
  0.0 95.7 jit_solution(495706719785088247)
XLA Ops:
  0.0 3.8 %turn_sum.2 = (f32[2,64,1024]{2,1,0:T(8,128)}, f32[2,64,1024]{2,1,0:T(8,128)}, f32[2,2,64,1024]{3,2,1,0:T(8,128)}) custom-call(s32[1]{0:T(128)} %bitcast.1.me_ref, s32[8]{0:T(128)} %group_ref.3, f32[8,1024]{1,0:T(8,128)} %phase_ref.3, f32[2,8,128,1024]{3,2,1,0:T(8,128)} %refl_ref.3), custom_call_target="tpu_custom_call" | custom-call | flops 320000000 | tf_op jit(solution)/shard_map/turn_sum/pallas_call | solution.py:247
  3.8 0.0 copy-start.7
  3.8 0.0 copy-start.8
  3.8 0.0 copy-start.2
  3.8 0.0 copy-start.5
  3.8 0.6 collective-permute-start
  4.4 3.9 %turn_sum.3 = (f32[2,64,1024]{2,1,0:T(8,128)}, f32[2,64,1024]{2,1,0:T(8,128)}, f32[2,2,64,1024]{3,2,1,0:T(8,128)}) custom-call(s32[1]{0:T(128)} %bitcast.1.me_ref, s32[8]{0:T(128)} %group_ref.3, f32[8,1024]{1,0:T(8,128)} %phase_ref.3, f32[2,8,128,1024]{3,2,1,0:T(8,128)} %refl_ref.3), custom_call_target="tpu_custom_call" | custom-call | flops 320000000 | tf_op jit(solution)/shard_map/turn_sum/pallas_call | solution.py:247
  8.3 0.1 collective-permute-start.6
  8.4 0.0 collective-permute-done
  8.4 0.0 copy-done.7
  8.4 0.0 copy-done.8
  8.4 0.0 copy-start.1
  8.4 0.0 copy-start.4
  8.5 0.9 fusion.2
  9.4 2.9 %collective-permute-start.1 = (f32[2,64,1024]{2,1,0:T(8,128)}, f32[2,64,1024]{2,1,0:T(8,128)}, u32[]{:S(2)}, u32[]{:S(2)}) collective-permute-start(f32[2,64,1024]{2,1,0:T(8,128)} %get-tuple-element.35), channel_id=1, source_target_pairs={{0,16},{8,24},{16,0},{24,8},{1,17},{9,25},{17,1},{25,9},{2,18},{10... | collective-permute-start | bytes 1572872 | tf_op jit(solution)/shard_map/ppermute | solution.py:499
  12.3 0.0 collective-permute-done.6
  12.3 2.1 %fusion = (f32[2,64,1024]{2,1,0:T(8,128)}, f32[2,64,1024]{2,1,0:T(8,128)S(1)}) fusion(f32[2,64,1024]{2,1,0:T(8,128)} %get-tuple-element.28, f32[2,2,64,1024]{3,2,1,0:T(8,128)S(1)} %collective-permute-done.6, f32[2,64,1024]{2,1,0:T(8,128)} %get-tuple-element.26), kind=kLoop, calls=%fused_computation.1 | loop fusion | flops 262144 | bytes 3145728 | tf_op jit(solution)/shard_map/add | solution.py:497
  14.4 0.0 copy-start
  14.4 0.0 copy-start.3
  14.4 1.5 %collective-permute-start.7 = (f32[2,64,1024]{2,1,0:T(8,128)}, f32[2,64,1024]{2,1,0:T(8,128)}, u32[]{:S(2)}, u32[]{:S(2)}) collective-permute-start(f32[2,64,1024]{2,1,0:T(8,128)} %get-tuple-element.33), channel_id=1, source_target_pairs={{0,16},{8,24},{16,0},{24,8},{1,17},{9,25},{17,1},{25,9},{2,18},{10... | collective-permute-start | bytes 1572872 | tf_op jit(solution)/shard_map/ppermute | solution.py:499
  15.9 9.4 %collective-permute-done.1.far_ref = f32[2,64,1024]{2,1,0:T(8,128)} collective-permute-done((f32[2,64,1024]{2,1,0:T(8,128)}, f32[2,64,1024]{2,1,0:T(8,128)}, u32[]{:S(2)}, u32[]{:S(2)}) %collective-permute-start.1) | collective-permute-done | bytes 524320 | tf_op jit(solution)/shard_map/ppermute | solution.py:499
  25.3 0.0 copy-done.2
  25.4 0.0 copy-done.5
  25.4 1.7 %columns_step.2 = (f32[2,128,128]{2,1,0:T(8,128)S(1)}, f32[2,128,128]{2,1,0:T(8,128)S(1)}, f32[2,128,128]{2,1,0:T(8,128)S(1)}, f32[2,128,128]{2,1,0:T(8,128)S(1)}) custom-call(s32[1]{0:T(128)} %bitcast.place_ref.origin_ref, bf16[256,1536]{1,0:T(8,128)(2,1)S(1)} %copy-done.2, f32[8,256]{1,0:T(8,128)S(1)} %copy-done.5, ...), custom_call_target="tpu_custom_call" | custom-call | flops 240000000 | tf_op jit(solution)/shard_map/columns_step/pallas_call | solution.py:311
  27.1 4.2 %collective-permute-start.4 = (f32[2,128,128]{2,1,0:T(8,128)S(1)}, f32[2,128,128]{2,1,0:T(8,128)S(1)}, u32[]{:S(2)}, u32[]{:S(2)}) collective-permute-start(f32[2,128,128]{2,1,0:T(8,128)S(1)} %get-tuple-element.25), channel_id=1, source_target_pairs={{0,6},{1,7},{2,4},{3,5},{4,2},{5,3},{6,0},{7,1},{8,14},{9,15},{10,... | collective-permute-start | bytes 393224 | tf_op jit(solution)/shard_map/ppermute | solution.py:505
  31.3 0.0 collective-permute-start.3
  31.3 0.6 collective-permute-start.2
  31.9 4.1 %collective-permute-done.7.far_ref = f32[2,64,1024]{2,1,0:T(8,128)} collective-permute-done((f32[2,64,1024]{2,1,0:T(8,128)}, f32[2,64,1024]{2,1,0:T(8,128)}, u32[]{:S(2)}, u32[]{:S(2)}) %collective-permute-start.7) | collective-permute-done | bytes 524320 | tf_op jit(solution)/shard_map/ppermute | solution.py:499
  36.0 1.7 %columns_step.3 = (f32[2,128,128]{2,1,0:T(8,128)S(1)}, f32[2,128,128]{2,1,0:T(8,128)S(1)}, f32[2,128,128]{2,1,0:T(8,128)S(1)}, f32[2,128,128]{2,1,0:T(8,128)S(1)}) custom-call(s32[1]{0:T(128)} %bitcast.place_ref.origin_ref, bf16[256,1536]{1,0:T(8,128)(2,1)S(1)} %copy-done.2, f32[8,256]{1,0:T(8,128)S(1)} %copy-done.5, ...), custom_call_target="tpu_custom_call" | custom-call | flops 240000000 | tf_op jit(solution)/shard_map/columns_step/pallas_call | solution.py:311
  37.8 3.9 %collective-permute-start.10 = (f32[2,128,128]{2,1,0:T(8,128)S(1)}, f32[2,128,128]{2,1,0:T(8,128)S(1)}, u32[]{:S(2)}, u32[]{:S(2)}) collective-permute-start(f32[2,128,128]{2,1,0:T(8,128)S(1)} %get-tuple-element.32), channel_id=1, source_target_pairs={{0,6},{1,7},{2,4},{3,5},{4,2},{5,3},{6,0},{7,1},{8,14},{9,15},{10,... | collective-permute-start | bytes 393224 | tf_op jit(solution)/shard_map/ppermute | solution.py:505
  41.7 0.0 collective-permute-start.9
  41.7 4.4 %collective-permute-done.10 = f32[2,128,128]{2,1,0:T(8,128)S(1)} collective-permute-done((f32[2,128,128]{2,1,0:T(8,128)S(1)}, f32[2,128,128]{2,1,0:T(8,128)S(1)}, u32[]{:S(2)}, u32[]{:S(2)}) %collective-permute-start.10) | collective-permute-done | bytes 131104 | tf_op jit(solution)/shard_map/ppermute | solution.py:505
  46.1 4.8 %collective-permute-start.8 = (f32[2,128,128]{2,1,0:T(8,128)S(1)}, f32[2,128,128]{2,1,0:T(8,128)S(1)}, u32[]{:S(2)}, u32[]{:S(2)}) collective-permute-start(f32[2,128,128]{2,1,0:T(8,128)S(1)} %get-tuple-element.30), channel_id=1, source_target_pairs={{0,2},{1,3},{2,0},{3,1},{4,6},{5,7},{6,4},{7,5},{8,10},{9,11},{10,... | collective-permute-start | bytes 393224 | tf_op jit(solution)/shard_map/ppermute | solution.py:505
  50.9 1.4 %collective-permute-done.9 = f32[2,128,128]{2,1,0:T(8,128)S(1)} collective-permute-done((f32[2,128,128]{2,1,0:T(8,128)S(1)}, f32[2,128,128]{2,1,0:T(8,128)S(1)}, u32[]{:S(2)}, u32[]{:S(2)}) %collective-permute-start.9) | collective-permute-done | bytes 131104 | tf_op jit(solution)/shard_map/ppermute | solution.py:505
  52.3 2.5 %collective-permute-done.8 = f32[2,128,128]{2,1,0:T(8,128)S(1)} collective-permute-done((f32[2,128,128]{2,1,0:T(8,128)S(1)}, f32[2,128,128]{2,1,0:T(8,128)S(1)}, u32[]{:S(2)}, u32[]{:S(2)}) %collective-permute-start.8) | collective-permute-done | bytes 131104 | tf_op jit(solution)/shard_map/ppermute | solution.py:505
  54.9 1.6 %collective-permute-start.13 = (f32[4,128,128]{2,1,0:T(8,128)S(1)}, f32[4,128,128]{2,1,0:T(8,128)S(1)}, u32[]{:S(2)}, u32[]{:S(2)}) collective-permute-start(f32[4,128,128]{2,1,0:T(8,128)S(1)} %pad_maximum_fusion.4.same_ref), channel_id=1, source_target_pairs={{0,1},{1,0},{2,3},{3,2},{4,5},{5,4},{6,7},{7,6},{8,9},{9,8},{10,11... | collective-permute-start | bytes 786440 | tf_op jit(solution)/shard_map/ppermute | solution.py:508
  56.4 0.0 collective-permute-done.4
  56.5 0.0 collective-permute-done.3
  56.5 0.0 collective-permute-done.2
  56.5 0.6 collective-permute-start.12
  57.2 6.9 %collective-permute-done.13.cross_ref = f32[4,128,128]{2,1,0:T(8,128)S(1)} collective-permute-done((f32[4,128,128]{2,1,0:T(8,128)S(1)}, f32[4,128,128]{2,1,0:T(8,128)S(1)}, u32[]{:S(2)}, u32[]{:S(2)}) %collective-permute-start.13) | collective-permute-done | bytes 262176 | tf_op jit(solution)/shard_map/ppermute | solution.py:508
  64.2 1.1 %collective-permute-start.15 = (f32[2,4,128,128]{3,2,1,0:T(8,128)S(1)}, f32[2,4,128,128]{3,2,1,0:T(8,128)S(1)}, u32[]{:S(2)}, u32[]{:S(2)}) collective-permute-start(f32[2,4,128,128]{3,2,1,0:T(8,128)S(1)} %pad_maximum_fusion.1), channel_id=1, source_target_pairs={{0,2},{1,7},{2,4},{3,1},{4,6},{5,3},{6,0},{7,5},{8,10},{9,15},{10,... | collective-permute-start | bytes 1572872 | tf_op jit(solution)/shard_map/ppermute | solution.py:510
  65.3 0.5 collective-permute-start.11
  65.8 3.9 %collective-permute-done.12.cross_ref = f32[4,128,128]{2,1,0:T(8,128)S(1)} collective-permute-done((f32[4,128,128]{2,1,0:T(8,128)S(1)}, f32[4,128,128]{2,1,0:T(8,128)S(1)}, u32[]{:S(2)}, u32[]{:S(2)}) %collective-permute-start.12) | collective-permute-done | bytes 262176 | tf_op jit(solution)/shard_map/ppermute | solution.py:508
  69.8 0.7 collective-permute-start.14
  70.5 1.1 %collective-permute-start.5 = (f32[4,128,128]{2,1,0:T(8,128)S(1)}, f32[4,128,128]{2,1,0:T(8,128)S(1)}, u32[]{:S(2)}, u32[]{:S(2)}) collective-permute-start(f32[4,128,128]{2,1,0:T(8,128)S(1)} %get-tuple-element.44.same_ref), channel_id=1, source_target_pairs={{0,1},{1,0},{2,3},{3,2},{4,5},{5,4},{6,7},{7,6},{8,9},{9,8},{10,11... | collective-permute-start | bytes 786440 | tf_op jit(solution)/shard_map/ppermute | solution.py:509
  71.6 0.0 copy-done.1
  71.6 0.0 copy-done.4
  71.6 0.8 rows_step.8.refs_0_
  72.4 0.0 copy-start.6
  72.4 3.0 %collective-permute-done.11.cross_ref = f32[4,128,128]{2,1,0:T(8,128)S(1)} collective-permute-done((f32[4,128,128]{2,1,0:T(8,128)S(1)}, f32[4,128,128]{2,1,0:T(8,128)S(1)}, u32[]{:S(2)}, u32[]{:S(2)}) %collective-permute-start.11) | collective-permute-done | bytes 262176 | tf_op jit(solution)/shard_map/ppermute | solution.py:509
  75.4 0.8 rows_step.6.refs_0_
  76.2 0.0 copy-done
  76.2 0.0 copy-done.3
  76.2 0.8 rows_step.9.near_in
  77.0 2.7 %collective-permute-done.5.cross_ref = f32[4,128,128]{2,1,0:T(8,128)S(1)} collective-permute-done((f32[4,128,128]{2,1,0:T(8,128)S(1)}, f32[4,128,128]{2,1,0:T(8,128)S(1)}, u32[]{:S(2)}, u32[]{:S(2)}) %collective-permute-start.5) | collective-permute-done | bytes 262176 | tf_op jit(solution)/shard_map/ppermute | solution.py:509
  79.7 0.8 rows_step.7.own_ref
  80.5 0.3 collective-permute-done.15
  80.8 0.8 rows_step.10.refs_0_
  81.6 7.0 %collective-permute-done.14 = f32[2,4,128,128]{3,2,1,0:T(8,128)S(1)} collective-permute-done((f32[2,4,128,128]{3,2,1,0:T(8,128)S(1)}, f32[2,4,128,128]{3,2,1,0:T(8,128)S(1)}, u32[]{:S(2)}, u32[]{:S(2)}) %collective-permute-start.14) | collective-permute-done | bytes 524320 | tf_op jit(solution)/shard_map/ppermute | solution.py:510
  88.7 0.8 rows_step.11.other_in
  89.5 0.0 copy-done.6
  89.5 6.1 %focus_step.1 = f32[2,1,1024,128]{3,2,1,0:T(8,128)} custom-call(s32[1]{0:T(128)} %bitcast.place_ref.origin_ref, s32[1,2]{1,0:T(1,128)S(1)} %copy-done.6, f32[2,1024,128]{2,1,0:T(8,128)S(1)} %rows_step.7.own_ref, f32[2,1024,128]{2,1,0:T(8,128)S(1)} %rows_step.9.near_in, f32[2,1024,128]{2,1,0:T(8,128)S(1)} %rows_step.11.other_in), custom_call_target="tpu_custom_call" | custom-call | flops 480000000 | tf_op jit(solution)/shard_map/focus_step/pallas_call | solution.py:460
  (16 shorter events, 0.3 us)
Async XLA Ops:
  3.8 4.6 %copy-start.7 = (f32[2,64,1024]{2,1,0:T(8,128)S(1)}, f32[2,64,1024]{2,1,0:T(8,128)}, u32[]{:S(2)}) copy-start(f32[2,64,1024]{2,1,0:T(8,128)} %get-tuple-element.19) | copy-start | bytes 1572868
  3.8 4.6 %copy-start.8 = (f32[2,64,1024]{2,1,0:T(8,128)S(1)}, f32[2,64,1024]{2,1,0:T(8,128)}, u32[]{:S(2)}) copy-start(f32[2,64,1024]{2,1,0:T(8,128)} %get-tuple-element.21) | copy-start | bytes 1572868
  3.8 21.5 %copy-start.2 = (bf16[256,1536]{1,0:T(8,128)(2,1)S(1)}, bf16[256,1536]{1,0:T(8,128)(2,1)}, u32[]{:S(2)}) copy-start(bf16[256,1536]{1,0:T(8,128)(2,1)} %constant.58.clone.table_ref) | copy-start | bytes 2359300
  3.8 21.5 %copy-start.5 = (f32[8,256]{1,0:T(8,128)S(1)}, f32[8,256]{1,0:T(8,128)}, u32[]{:S(2)}) copy-start(f32[8,256]{1,0:T(8,128)} %constant.59.clone.turn_ref) | copy-start | bytes 24580
  3.8 4.6 %collective-permute-start = (f32[2,2,64,1024]{3,2,1,0:T(8,128)}, f32[2,2,64,1024]{3,2,1,0:T(8,128)S(1)}, u32[]{:S(2)}, u32[]{:S(2)}) collective-permute-start(f32[2,2,64,1024]{3,2,1,0:T(8,128)} %get-tuple-element.20), channel_id=1, source_target_pairs={{0,8},{8,0},{16,24},{24,16},{1,9},{9,1},{17,25},{25,17},{2,10},{10... | collective-permute-start | bytes 3145736 | tf_op jit(solution)/shard_map/ppermute | solution.py:496
  8.3 4.0 %collective-permute-start.6 = (f32[2,2,64,1024]{3,2,1,0:T(8,128)}, f32[2,2,64,1024]{3,2,1,0:T(8,128)S(1)}, u32[]{:S(2)}, u32[]{:S(2)}) collective-permute-start(f32[2,2,64,1024]{3,2,1,0:T(8,128)} %get-tuple-element.27), channel_id=1, source_target_pairs={{0,8},{8,0},{16,24},{24,16},{1,9},{9,1},{17,25},{25,17},{2,10},{10... | collective-permute-start | bytes 3145736 | tf_op jit(solution)/shard_map/ppermute | solution.py:496
  8.4 63.1 %copy-start.1 = (bf16[512,768]{1,0:T(8,128)(2,1)S(1)}, bf16[512,768]{1,0:T(8,128)(2,1)}, u32[]{:S(2)}) copy-start(bf16[512,768]{1,0:T(8,128)(2,1)} %constant.60.clone.table_ref) | copy-start | bytes 2359300
  8.4 63.1 %copy-start.4 = (f32[8,256]{1,0:T(8,128)S(1)}, f32[8,256]{1,0:T(8,128)}, u32[]{:S(2)}) copy-start(f32[8,256]{1,0:T(8,128)} %constant.61.clone.turn_ref) | copy-start | bytes 24580
  9.4 16.0 %collective-permute-start.1 = (f32[2,64,1024]{2,1,0:T(8,128)}, f32[2,64,1024]{2,1,0:T(8,128)}, u32[]{:S(2)}, u32[]{:S(2)}) collective-permute-start(f32[2,64,1024]{2,1,0:T(8,128)} %get-tuple-element.35), channel_id=1, source_target_pairs={{0,16},{8,24},{16,0},{24,8},{1,17},{9,25},{17,1},{25,9},{2,18},{10... | collective-permute-start | bytes 1572872 | tf_op jit(solution)/shard_map/ppermute | solution.py:499
  14.4 61.8 %copy-start = (bf16[512,768]{1,0:T(8,128)(2,1)S(1)}, bf16[512,768]{1,0:T(8,128)(2,1)}, u32[]{:S(2)}) copy-start(bf16[512,768]{1,0:T(8,128)(2,1)} %constant.62.clone.table_ref) | copy-start | bytes 2359300
  14.4 61.8 %copy-start.3 = (f32[8,256]{1,0:T(8,128)S(1)}, f32[8,256]{1,0:T(8,128)}, u32[]{:S(2)}) copy-start(f32[8,256]{1,0:T(8,128)} %constant.63.clone.turn_ref) | copy-start | bytes 24580
  14.4 21.7 %collective-permute-start.7 = (f32[2,64,1024]{2,1,0:T(8,128)}, f32[2,64,1024]{2,1,0:T(8,128)}, u32[]{:S(2)}, u32[]{:S(2)}) collective-permute-start(f32[2,64,1024]{2,1,0:T(8,128)} %get-tuple-element.33), channel_id=1, source_target_pairs={{0,16},{8,24},{16,0},{24,8},{1,17},{9,25},{17,1},{25,9},{2,18},{10... | collective-permute-start | bytes 1572872 | tf_op jit(solution)/shard_map/ppermute | solution.py:499
  27.1 29.3 %collective-permute-start.4 = (f32[2,128,128]{2,1,0:T(8,128)S(1)}, f32[2,128,128]{2,1,0:T(8,128)S(1)}, u32[]{:S(2)}, u32[]{:S(2)}) collective-permute-start(f32[2,128,128]{2,1,0:T(8,128)S(1)} %get-tuple-element.25), channel_id=1, source_target_pairs={{0,6},{1,7},{2,4},{3,5},{4,2},{5,3},{6,0},{7,1},{8,14},{9,15},{10,... | collective-permute-start | bytes 393224 | tf_op jit(solution)/shard_map/ppermute | solution.py:505
  31.3 25.2 %collective-permute-start.3 = (f32[2,128,128]{2,1,0:T(8,128)S(1)}, f32[2,128,128]{2,1,0:T(8,128)S(1)}, u32[]{:S(2)}, u32[]{:S(2)}) collective-permute-start(f32[2,128,128]{2,1,0:T(8,128)S(1)} %get-tuple-element.24), channel_id=1, source_target_pairs={{0,4},{1,5},{2,6},{3,7},{4,0},{5,1},{6,2},{7,3},{8,12},{9,13},{10,... | collective-permute-start | bytes 393224 | tf_op jit(solution)/shard_map/ppermute | solution.py:505
  31.3 25.2 %collective-permute-start.2 = (f32[2,128,128]{2,1,0:T(8,128)S(1)}, f32[2,128,128]{2,1,0:T(8,128)S(1)}, u32[]{:S(2)}, u32[]{:S(2)}) collective-permute-start(f32[2,128,128]{2,1,0:T(8,128)S(1)} %get-tuple-element.23), channel_id=1, source_target_pairs={{0,2},{1,3},{2,0},{3,1},{4,6},{5,7},{6,4},{7,5},{8,10},{9,11},{10,... | collective-permute-start | bytes 393224 | tf_op jit(solution)/shard_map/ppermute | solution.py:505
  37.8 8.3 %collective-permute-start.10 = (f32[2,128,128]{2,1,0:T(8,128)S(1)}, f32[2,128,128]{2,1,0:T(8,128)S(1)}, u32[]{:S(2)}, u32[]{:S(2)}) collective-permute-start(f32[2,128,128]{2,1,0:T(8,128)S(1)} %get-tuple-element.32), channel_id=1, source_target_pairs={{0,6},{1,7},{2,4},{3,5},{4,2},{5,3},{6,0},{7,1},{8,14},{9,15},{10,... | collective-permute-start | bytes 393224 | tf_op jit(solution)/shard_map/ppermute | solution.py:505
  41.7 10.6 %collective-permute-start.9 = (f32[2,128,128]{2,1,0:T(8,128)S(1)}, f32[2,128,128]{2,1,0:T(8,128)S(1)}, u32[]{:S(2)}, u32[]{:S(2)}) collective-permute-start(f32[2,128,128]{2,1,0:T(8,128)S(1)} %get-tuple-element.31), channel_id=1, source_target_pairs={{0,4},{1,5},{2,6},{3,7},{4,0},{5,1},{6,2},{7,3},{8,12},{9,13},{10,... | collective-permute-start | bytes 393224 | tf_op jit(solution)/shard_map/ppermute | solution.py:505
  46.1 8.8 %collective-permute-start.8 = (f32[2,128,128]{2,1,0:T(8,128)S(1)}, f32[2,128,128]{2,1,0:T(8,128)S(1)}, u32[]{:S(2)}, u32[]{:S(2)}) collective-permute-start(f32[2,128,128]{2,1,0:T(8,128)S(1)} %get-tuple-element.30), channel_id=1, source_target_pairs={{0,2},{1,3},{2,0},{3,1},{4,6},{5,7},{6,4},{7,5},{8,10},{9,11},{10,... | collective-permute-start | bytes 393224 | tf_op jit(solution)/shard_map/ppermute | solution.py:505
  54.9 9.2 %collective-permute-start.13 = (f32[4,128,128]{2,1,0:T(8,128)S(1)}, f32[4,128,128]{2,1,0:T(8,128)S(1)}, u32[]{:S(2)}, u32[]{:S(2)}) collective-permute-start(f32[4,128,128]{2,1,0:T(8,128)S(1)} %pad_maximum_fusion.4.same_ref), channel_id=1, source_target_pairs={{0,1},{1,0},{2,3},{3,2},{4,5},{5,4},{6,7},{7,6},{8,9},{9,8},{10,11... | collective-permute-start | bytes 786440 | tf_op jit(solution)/shard_map/ppermute | solution.py:508
  56.5 13.2 %collective-permute-start.12 = (f32[4,128,128]{2,1,0:T(8,128)S(1)}, f32[4,128,128]{2,1,0:T(8,128)S(1)}, u32[]{:S(2)}, u32[]{:S(2)}) collective-permute-start(f32[4,128,128]{2,1,0:T(8,128)S(1)} %pad_maximum_fusion.2.same_ref), channel_id=1, source_target_pairs={{0,1},{1,0},{2,3},{3,2},{4,5},{5,4},{6,7},{7,6},{8,9},{9,8},{10,11... | collective-permute-start | bytes 786440 | tf_op jit(solution)/shard_map/ppermute | solution.py:508
  64.2 16.6 %collective-permute-start.15 = (f32[2,4,128,128]{3,2,1,0:T(8,128)S(1)}, f32[2,4,128,128]{3,2,1,0:T(8,128)S(1)}, u32[]{:S(2)}, u32[]{:S(2)}) collective-permute-start(f32[2,4,128,128]{3,2,1,0:T(8,128)S(1)} %pad_maximum_fusion.1), channel_id=1, source_target_pairs={{0,2},{1,7},{2,4},{3,1},{4,6},{5,3},{6,0},{7,5},{8,10},{9,15},{10,... | collective-permute-start | bytes 1572872 | tf_op jit(solution)/shard_map/ppermute | solution.py:510
  65.3 10.1 %collective-permute-start.11 = (f32[4,128,128]{2,1,0:T(8,128)S(1)}, f32[4,128,128]{2,1,0:T(8,128)S(1)}, u32[]{:S(2)}, u32[]{:S(2)}) collective-permute-start(f32[4,128,128]{2,1,0:T(8,128)S(1)} %get-tuple-element.42.same_ref), channel_id=1, source_target_pairs={{0,1},{1,0},{2,3},{3,2},{4,5},{5,4},{6,7},{7,6},{8,9},{9,8},{10,11... | collective-permute-start | bytes 786440 | tf_op jit(solution)/shard_map/ppermute | solution.py:509
  69.8 18.9 %collective-permute-start.14 = (f32[2,4,128,128]{3,2,1,0:T(8,128)S(1)}, f32[2,4,128,128]{3,2,1,0:T(8,128)S(1)}, u32[]{:S(2)}, u32[]{:S(2)}) collective-permute-start(f32[2,4,128,128]{3,2,1,0:T(8,128)S(1)} %pad_maximum_fusion), channel_id=1, source_target_pairs={{0,2},{1,7},{2,4},{3,1},{4,6},{5,3},{6,0},{7,5},{8,10},{9,15},{10,... | collective-permute-start | bytes 1572872 | tf_op jit(solution)/shard_map/ppermute | solution.py:510
  70.5 9.3 %collective-permute-start.5 = (f32[4,128,128]{2,1,0:T(8,128)S(1)}, f32[4,128,128]{2,1,0:T(8,128)S(1)}, u32[]{:S(2)}, u32[]{:S(2)}) collective-permute-start(f32[4,128,128]{2,1,0:T(8,128)S(1)} %get-tuple-element.44.same_ref), channel_id=1, source_target_pairs={{0,1},{1,0},{2,3},{3,2},{4,5},{5,4},{6,7},{7,6},{8,9},{9,8},{10,11... | collective-permute-start | bytes 786440 | tf_op jit(solution)/shard_map/ppermute | solution.py:509
  72.4 17.1 %copy-start.6 = (s32[1,2]{1,0:T(1,128)S(1)}, s32[1,2]{1,0:T(1,128)}, u32[]{:S(2)}) copy-start(s32[1,2]{1,0:T(1,128)} %widths_ref.1) | copy-start | bytes 28

commit v2 on v1

--- a/solution.py
+++ b/solution.py
@@ -195,7 +195,7 @@
     twist = [unit_angles(row * k, width) for k in range(4)]
     sign = np.where(imaginary, 1.0, -1.0)
     turn = np.stack([t[0] for t in twist] + [t[1] * sign for t in twist])
-    return halves(np.concatenate([upper, lower], axis=0)), jnp.asarray(turn, F32)
+    return halves(np.concatenate([upper, lower], axis=0)).T, jnp.asarray(turn, F32)
 
 
 def split(value):
@@ -323,7 +323,7 @@
 def rows_kernel(origin_ref, table_ref, turn_ref, same_ref, cross_ref, *refs):
     out_ref, pieces_ref = refs[-2:]
     spaces, block, _ = pieces_ref.shape
-    quarter = out_ref.shape[1] // 4
+    quarter = out_ref.shape[3]
     origin = origin_ref[0]
     for k in range(spaces // 2):
         pieces_ref[origin ^ (2 * k)] = same_ref[k]
@@ -350,14 +350,14 @@
             mixed[k].append(v)
     for pair in range(2):
         stacked = [jnp.concatenate(mixed[k], axis=1) for k in (2 * pair, 2 * pair + 1)]
-        out = product(table_ref[...], jnp.concatenate(stacked, axis=0))
+        high, low = split(jnp.concatenate(stacked, axis=0))
+        out = jnp.dot(jnp.concatenate([high, low, high], axis=1), table_ref[...], preferred_element_type=F32)
         for e in range(2):
-            at = pl.ds(2 * pair + e, quarter, stride=4)
             for p in range(2):
-                value = out[p * quarter : (p + 1) * quarter, e * block : (e + 1) * block]
+                value = out[e * block : (e + 1) * block, p * quarter : (p + 1) * quarter]
                 if len(refs) > 2:
-                    value = value + refs[0][p, at, :]
-                out_ref[p, at, :] = value
+                    value = value + refs[0][2 * pair + e, p]
+                out_ref[2 * pair + e, p] = value
 
 
 def rows_step(origin, tables, same, cross, *sofar):
@@ -367,7 +367,7 @@
         rows_kernel,
         in_specs=[pl.BlockSpec(memory_space=pltpu.SMEM)] + [pl.BlockSpec(memory_space=pltpu.VMEM)] * (4 + len(sofar)),
         out_specs=pl.BlockSpec(memory_space=pltpu.VMEM),
-        out_shape=jax.ShapeDtypeStruct((2, width, block), F32),
+        out_shape=jax.ShapeDtypeStruct((4, 2, block, width // 4), F32),
         scratch_shapes=[pltpu.VMEM((2 * pairs, block, block), F32)],
         name="rows_step",
         compiler_params=pltpu.CompilerParams(vmem_limit_bytes=12 * 2**20),
@@ -375,98 +375,101 @@
     )(origin, *tables, same, cross, *sofar)
 
 
-def focus_kernel(place_ref, widths_ref, own_ref, near_in, other_in, out_ref, near_ref, other_ref):
-    rows, block = own_ref.shape[1:]
+def focus_kernel(place_ref, origin_ref, widths_ref, table_ref, turn_ref, own_ref, near_ref, same_ref, cross_ref, *refs):
+    sofar_ref, out_ref, other_ref, pieces_ref, vector_ref = refs
+    rows_kernel(origin_ref, table_ref, turn_ref, same_ref, cross_ref, sofar_ref, other_ref, pieces_ref)
+    _, _, block, quarter = own_ref.shape
+    rows = 4 * quarter
     step = 128
-    tiles = rows // step
-    position = lax.broadcasted_iota(jnp.int32, (1, block), 1)
+    places = [(k, h) for k in range(4) for h in range(0, quarter, step)]
     near_left = place_ref[0] % 2
-    left = (position >= block - widths_ref[0, 0]).astype(jnp.int32)
-    right = (position < widths_ref[0, 1]).astype(jnp.int32)
-    near = (left * near_left + right * (1 - near_left)).astype(F32)
-    other = (right * near_left + left * (1 - near_left)).astype(F32)
-
-    def masks(t, carry):
-        at = pl.ds(pl.multiple_of(t * step, step), step)
-        for p in range(2):
-            near_ref[p, at, :] = near_in[p, at, :] * near
-            other_ref[p, at, :] = other_in[p, at, :] * other
+
+    def keep(top):
+        position = top + lax.broadcasted_iota(jnp.int32, (8, 1), 0)
+        left = (position >= block - widths_ref[0, 0]).astype(jnp.int32)
+        right = (position < widths_ref[0, 1]).astype(jnp.int32)
+        near = (left * near_left + right * (1 - near_left)).astype(F32)
+        other = (right * near_left + left * (1 - near_left)).astype(F32)
+        return near, other
+
+    groups = []
+    for top in range(0, block, 8):
+        near, other = keep(top)
+        groups += [(own_ref, top, None), (near_ref, top, near), (other_ref, top, other)]
+
+    def plane(ref, top, p):
+        return [ref[k, p, top : top + 8, h : h + step] for k, h in places]
+
+    def normalize_rows(reals, imags):
+        reals = [jnp.sum(x, axis=0, keepdims=True) for x in reals]
+        imags = [jnp.sum(x, axis=0, keepdims=True) for x in imags]
+        powers = [r * r + i * i for r, i in zip(reals, imags)]
+        total = jnp.sum(sum(powers[1:], powers[0]), axis=1, keepdims=True)
+        for t, power in enumerate(powers):
+            scale = lax.rsqrt(power + total / rows + 1e-06)
+            vector_ref[0, t : t + 1, :] = reals[t] * scale
+            vector_ref[1, t : t + 1, :] = imags[t] * scale
+
+    def vectors(p):
+        return [jnp.broadcast_to(vector_ref[p, t : t + 1, :], (8, step)) for t in range(len(places))]
+
+    zeros = [jnp.zeros((8, step), F32) for _ in places]
+    real, imag = list(zeros), list(zeros)
+    for ref, top, mask in groups:
+        for total, p in ((real, 0), (imag, 1)):
+            for t, x in enumerate(plane(ref, top, p)):
+                total[t] = total[t] + (x if mask is None else x * mask)
+    normalize_rows(real, imag)
+
+    def iterate(_, carry):
+        v_r, v_i = vectors(0), vectors(1)
+        real, imag = list(zeros), list(zeros)
+        for ref, top, mask in groups:
+            r, i = plane(ref, top, 0), plane(ref, top, 1)
+            b_r = sum(x * u + y * v for x, y, u, v in zip(r, i, v_r, v_i))
+            b_i = sum(x * v - y * u for x, y, u, v in zip(r, i, v_r, v_i))
+            b_r = jnp.sum(b_r, axis=1, keepdims=True)
+            b_i = jnp.sum(b_i, axis=1, keepdims=True)
+            if mask is not None:
+                b_r, b_i = b_r * mask, b_i * mask
+            b_r = jnp.broadcast_to(b_r, (8, step))
+            b_i = jnp.broadcast_to(b_i, (8, step))
+            for t in range(len(places)):
+                real[t] = real[t] + (r[t] * b_r - i[t] * b_i)
+                imag[t] = imag[t] + (r[t] * b_i + i[t] * b_r)
+        normalize_rows(real, imag)
         return carry
 
-    lax.fori_loop(0, tiles, masks, 0)
-    blocks = (near_ref, own_ref, other_ref)
-
-    def normal(real, imag, total):
-        power = real * real + imag * imag
-        scale = lax.rsqrt(power + total / rows + 1e-06)
-        return real * scale, imag * scale
-
-    def tile(ref, t):
-        return ref[0, t * step : (t + 1) * step, :], ref[1, t * step : (t + 1) * step, :]
-
-    def reduce_rows(parts):
-        reals, imags = [], []
-        total = jnp.zeros((1, 1), F32)
-        for real, imag in parts:
-            real = jnp.sum(real, axis=1, keepdims=True)
-            imag = jnp.sum(imag, axis=1, keepdims=True)
-            total = total + jnp.sum(real * real + imag * imag, axis=0, keepdims=True)
-            reals.append(real)
-            imags.append(imag)
-        return [normal(r, i, total) for r, i in zip(reals, imags)]
-
-    def first():
-        for t in range(tiles):
-            real = near_ref[0, t * step : (t + 1) * step, :]
-            imag = near_ref[1, t * step : (t + 1) * step, :]
-            for ref in blocks[1:]:
-                r, i = tile(ref, t)
-                real, imag = real + r, imag + i
-            yield real, imag
-
-    vector = reduce_rows(first())
-    for _ in range(ITERS):
-        back = []
-        for ref in blocks:
-            back_r = jnp.zeros((8, block), F32)
-            back_i = jnp.zeros((8, block), F32)
-            for t in range(tiles):
-                r, i = tile(ref, t)
-                v_r, v_i = vector[t]
-                back_r += jnp.sum((r * v_r + i * v_i).reshape(step // 8, 8, block), axis=0)
-                back_i += jnp.sum((r * v_i - i * v_r).reshape(step // 8, 8, block), axis=0)
-            back.append((jnp.sum(back_r, axis=0, keepdims=True), jnp.sum(back_i, axis=0, keepdims=True)))
-
-        def forward():
-            for t in range(tiles):
-                real = imag = None
-                for ref, (b_r, b_i) in zip(blocks, back):
-                    r, i = tile(ref, t)
-                    x, y = r * b_r - i * b_i, r * b_i + i * b_r
-                    real, imag = (x, y) if real is None else (real + x, imag + y)
-                yield real, imag
-
-        vector = reduce_rows(forward())
-    for t in range(tiles):
-        r, i = tile(own_ref, t)
-        v_r, v_i = vector[t]
-        out_ref[0, 0, t * step : (t + 1) * step, :] = v_r * r + v_i * i
-        out_ref[1, 0, t * step : (t + 1) * step, :] = v_r * i - v_i * r
-
-
-def focus_step(place, widths, own, near, other):
-    _, rows, block = own.shape
+    lax.fori_loop(0, ITERS, iterate, 0)
+    for t, (k, h) in enumerate(places):
+        r = own_ref[k, 0, :, h : h + step]
+        i = own_ref[k, 1, :, h : h + step]
+        v_r = vector_ref[0, t : t + 1, :]
+        v_i = vector_ref[1, t : t + 1, :]
+        at = pl.ds(4 * h + k, step, stride=4)
+        out_ref[0, 0, at, :] = (v_r * r + v_i * i).T
+        out_ref[1, 0, at, :] = (v_r * i - v_i * r).T
+
+
+def focus_step(place, origin, widths, tables, own, near, same, cross, sofar):
+    _, _, block, quarter = own.shape
+    rows = 4 * quarter
+    smem = pl.BlockSpec(memory_space=pltpu.SMEM)
     vmem = pl.BlockSpec(memory_space=pltpu.VMEM)
     return pl.pallas_call(
         focus_kernel,
-        in_specs=[pl.BlockSpec(memory_space=pltpu.SMEM)] * 2 + [vmem] * 3,
+        in_specs=[smem] * 3 + [vmem] * 7,
         out_specs=vmem,
         out_shape=jax.ShapeDtypeStruct((2, 1, rows, block), F32),
-        scratch_shapes=[pltpu.VMEM((2, rows, block), F32), pltpu.VMEM((2, rows, block), F32)],
+        scratch_shapes=[
+            pltpu.VMEM(own.shape, F32),
+            pltpu.VMEM((rows // block, block, block), F32),
+            pltpu.VMEM((2, rows // 128, 128), F32),
+        ],
         name="focus_step",
         compiler_params=pltpu.CompilerParams(vmem_limit_bytes=16 * 2**20),
         cost_estimate=cost(6),
-    )(place, widths, own, near, other)
+    )(place, origin, widths, *tables, own, near, same, cross, sofar)
 
 
 CHUNKS = 2
@@ -510,8 +513,11 @@
         beyond = lax.ppermute(jnp.stack([near_same, near_cross]), "space", along)
         own_block = (rows_step(place, rows, own_same, own_cross, *own_block),)
         near_block = (rows_step(place, rows, near_same, near_cross, *near_block),)
-        other_block = (rows_step(beyond_from, rows, beyond[0], beyond[1], *other_block),)
-    return focus_step(place, widths, own_block[0], near_block[0], other_block[0])
+        if h + 1 < CHUNKS:
+            other_block = (rows_step(beyond_from, rows, beyond[0], beyond[1], *other_block),)
+    return focus_step(
+        place, beyond_from, widths, rows, own_block[0], near_block[0], beyond[0], beyond[1], other_block[0]
+    )
 
 
 def solution(mesh):

time: 95.9 us -> 94.7 us (0.987)
  Pallas kernels: 22.1 us -> 20.5 us
    pallas_call x6 -> x5, Pallas kernels: 4.75 us -> 3.62 us  [rows_step(): pl.pallas_call(rows_kernel, in_specs=[pl.BlockSpec(memory_space=pltpu.SME...]
  transfers between devices with their start and end apart: 16 -> 16, of which waited for: 11 -> 11; matrix products, arithmetic and copies ran while one was open for 3% -> 4% of each run, Pallas kernels for 12% -> 12%
where the time goes in v2:
time: 94.7 us; the launch traced here: 94.5 us
  waiting for transfers between devices  46.2 us (49%)
  starting transfers between devices  24 us (25%)
  Pallas kernels  20.5 us (22%)
  other arithmetic  3.23 us (3%)
    ppermute x2, waiting for transfers between devices, focus_all(): fars.append(lax.ppermute(partial, 'freq', far))  13.5 us
    ppermute x6, starting transfers between devices, focus_all(): lax.ppermute(pieces[k], 'space', [(i, i ^ 2 * k) for i in range(spaces)])  13.5 us
    ppermute x2, waiting for transfers between devices, focus_all(): near_cross = lax.ppermute(own_same, 'space', across)  10.9 us
    ppermute x6, waiting for transfers between devices, focus_all(): lax.ppermute(pieces[k], 'space', [(i, i ^ 2 * k) for i in range(spaces)])  8.31 us
    pallas_call x2, Pallas kernels, turn_sum(): pl.pallas_call(turn_kernel, grid=(rows // rows_at,), in_specs=[pl.BlockSp...  7.69 us
    ppermute x2, waiting for transfers between devices, focus_all(): beyond = lax.ppermute(jnp.stack([near_same, near_cross]), 'space', along)  7.44 us
    ppermute x2, waiting for transfers between devices, focus_all(): own_cross = lax.ppermute(near_same, 'space', across)  6.09 us
    pallas_call x1, Pallas kernels, focus_step(): pl.pallas_call(focus_kernel, in_specs=[smem] * 3 + [vmem] * 7, out_specs=...  5.75 us
  transfers between devices with their start and end apart: 16, of which 11 were waited for; matrix products, arithmetic and copies ran while one was open for 4% of the time, Pallas kernels for 12%

profile of v2, /device:TPU:0, one launch (start us, length us, event | category | flops | bytes accessed | tf_op | source)
XLA Modules:
  0.0 94.5 jit_solution(1041116062209547478)
XLA Ops:
  0.0 3.8 %turn_sum.2 = (f32[2,64,1024]{2,1,0:T(8,128)}, f32[2,64,1024]{2,1,0:T(8,128)}, f32[2,2,64,1024]{3,2,1,0:T(8,128)}) custom-call(s32[1]{0:T(128)} %bitcast.1.me_ref, s32[8]{0:T(128)} %group_ref.3, f32[8,1024]{1,0:T(8,128)} %phase_ref.3, f32[2,8,128,1024]{3,2,1,0:T(8,128)} %refl_ref.3), custom_call_target="tpu_custom_call" | custom-call | flops 320000000 | tf_op jit(solution)/shard_map/turn_sum/pallas_call | solution.py:247
  3.8 0.0 copy-start.7
  3.8 0.0 copy-start.8
  3.8 0.0 copy-start.2
  3.8 0.0 copy-start.5
  3.8 0.6 collective-permute-start
  4.4 3.9 %turn_sum.3 = (f32[2,64,1024]{2,1,0:T(8,128)}, f32[2,64,1024]{2,1,0:T(8,128)}, f32[2,2,64,1024]{3,2,1,0:T(8,128)}) custom-call(s32[1]{0:T(128)} %bitcast.1.me_ref, s32[8]{0:T(128)} %group_ref.3, f32[8,1024]{1,0:T(8,128)} %phase_ref.3, f32[2,8,128,1024]{3,2,1,0:T(8,128)} %refl_ref.3), custom_call_target="tpu_custom_call" | custom-call | flops 320000000 | tf_op jit(solution)/shard_map/turn_sum/pallas_call | solution.py:247
  8.3 0.1 collective-permute-start.6
  8.4 0.0 collective-permute-done
  8.4 0.0 copy-done.7
  8.4 0.0 copy-done.8
  8.4 0.0 copy-start.1
  8.4 0.0 copy-start.4
  8.5 0.9 fusion.2
  9.4 2.9 %collective-permute-start.1 = (f32[2,64,1024]{2,1,0:T(8,128)}, f32[2,64,1024]{2,1,0:T(8,128)}, u32[]{:S(2)}, u32[]{:S(2)}) collective-permute-start(f32[2,64,1024]{2,1,0:T(8,128)} %get-tuple-element.35), channel_id=1, source_target_pairs={{0,16},{8,24},{16,0},{24,8},{1,17},{9,25},{17,1},{25,9},{2,18},{10... | collective-permute-start | bytes 1572872 | tf_op jit(solution)/shard_map/ppermute | solution.py:502
  12.3 0.0 collective-permute-done.6
  12.3 2.1 %fusion = (f32[2,64,1024]{2,1,0:T(8,128)}, f32[2,64,1024]{2,1,0:T(8,128)S(1)}) fusion(f32[2,64,1024]{2,1,0:T(8,128)} %get-tuple-element.28, f32[2,2,64,1024]{3,2,1,0:T(8,128)S(1)} %collective-permute-done.6, f32[2,64,1024]{2,1,0:T(8,128)} %get-tuple-element.26), kind=kLoop, calls=%fused_computation.1 | loop fusion | flops 262144 | bytes 3145728 | tf_op jit(solution)/shard_map/add | solution.py:500
  14.4 0.0 copy-start
  14.4 0.0 copy-start.3
  14.4 1.5 %collective-permute-start.7 = (f32[2,64,1024]{2,1,0:T(8,128)}, f32[2,64,1024]{2,1,0:T(8,128)}, u32[]{:S(2)}, u32[]{:S(2)}) collective-permute-start(f32[2,64,1024]{2,1,0:T(8,128)} %get-tuple-element.33), channel_id=1, source_target_pairs={{0,16},{8,24},{16,0},{24,8},{1,17},{9,25},{17,1},{25,9},{2,18},{10... | collective-permute-start | bytes 1572872 | tf_op jit(solution)/shard_map/ppermute | solution.py:502
  15.9 9.4 %collective-permute-done.1.far_ref = f32[2,64,1024]{2,1,0:T(8,128)} collective-permute-done((f32[2,64,1024]{2,1,0:T(8,128)}, f32[2,64,1024]{2,1,0:T(8,128)}, u32[]{:S(2)}, u32[]{:S(2)}) %collective-permute-start.1) | collective-permute-done | bytes 524320 | tf_op jit(solution)/shard_map/ppermute | solution.py:502
  25.3 0.0 copy-done.2
  25.4 0.0 copy-done.5
  25.4 1.7 %columns_step.2 = (f32[2,128,128]{2,1,0:T(8,128)S(1)}, f32[2,128,128]{2,1,0:T(8,128)S(1)}, f32[2,128,128]{2,1,0:T(8,128)S(1)}, f32[2,128,128]{2,1,0:T(8,128)S(1)}) custom-call(s32[1]{0:T(128)} %bitcast.place_ref.origin_ref, bf16[256,1536]{1,0:T(8,128)(2,1)S(1)} %copy-done.2, f32[8,256]{1,0:T(8,128)S(1)} %copy-done.5, ...), custom_call_target="tpu_custom_call" | custom-call | flops 240000000 | tf_op jit(solution)/shard_map/columns_step/pallas_call | solution.py:311
  27.1 4.2 %collective-permute-start.4 = (f32[2,128,128]{2,1,0:T(8,128)S(1)}, f32[2,128,128]{2,1,0:T(8,128)S(1)}, u32[]{:S(2)}, u32[]{:S(2)}) collective-permute-start(f32[2,128,128]{2,1,0:T(8,128)S(1)} %get-tuple-element.25), channel_id=1, source_target_pairs={{0,6},{1,7},{2,4},{3,5},{4,2},{5,3},{6,0},{7,1},{8,14},{9,15},{10,... | collective-permute-start | bytes 393224 | tf_op jit(solution)/shard_map/ppermute | solution.py:508
  31.3 0.0 collective-permute-start.3
  31.3 0.6 collective-permute-start.2
  31.9 4.1 %collective-permute-done.7.far_ref = f32[2,64,1024]{2,1,0:T(8,128)} collective-permute-done((f32[2,64,1024]{2,1,0:T(8,128)}, f32[2,64,1024]{2,1,0:T(8,128)}, u32[]{:S(2)}, u32[]{:S(2)}) %collective-permute-start.7) | collective-permute-done | bytes 524320 | tf_op jit(solution)/shard_map/ppermute | solution.py:502
  36.0 1.7 %columns_step.3 = (f32[2,128,128]{2,1,0:T(8,128)S(1)}, f32[2,128,128]{2,1,0:T(8,128)S(1)}, f32[2,128,128]{2,1,0:T(8,128)S(1)}, f32[2,128,128]{2,1,0:T(8,128)S(1)}) custom-call(s32[1]{0:T(128)} %bitcast.place_ref.origin_ref, bf16[256,1536]{1,0:T(8,128)(2,1)S(1)} %copy-done.2, f32[8,256]{1,0:T(8,128)S(1)} %copy-done.5, ...), custom_call_target="tpu_custom_call" | custom-call | flops 240000000 | tf_op jit(solution)/shard_map/columns_step/pallas_call | solution.py:311
  37.8 3.9 %collective-permute-start.10 = (f32[2,128,128]{2,1,0:T(8,128)S(1)}, f32[2,128,128]{2,1,0:T(8,128)S(1)}, u32[]{:S(2)}, u32[]{:S(2)}) collective-permute-start(f32[2,128,128]{2,1,0:T(8,128)S(1)} %get-tuple-element.32), channel_id=1, source_target_pairs={{0,6},{1,7},{2,4},{3,5},{4,2},{5,3},{6,0},{7,1},{8,14},{9,15},{10,... | collective-permute-start | bytes 393224 | tf_op jit(solution)/shard_map/ppermute | solution.py:508
  41.7 0.0 collective-permute-start.9
  41.7 4.4 %collective-permute-done.10 = f32[2,128,128]{2,1,0:T(8,128)S(1)} collective-permute-done((f32[2,128,128]{2,1,0:T(8,128)S(1)}, f32[2,128,128]{2,1,0:T(8,128)S(1)}, u32[]{:S(2)}, u32[]{:S(2)}) %collective-permute-start.10) | collective-permute-done | bytes 131104 | tf_op jit(solution)/shard_map/ppermute | solution.py:508
  46.1 4.8 %collective-permute-start.8 = (f32[2,128,128]{2,1,0:T(8,128)S(1)}, f32[2,128,128]{2,1,0:T(8,128)S(1)}, u32[]{:S(2)}, u32[]{:S(2)}) collective-permute-start(f32[2,128,128]{2,1,0:T(8,128)S(1)} %get-tuple-element.30), channel_id=1, source_target_pairs={{0,2},{1,3},{2,0},{3,1},{4,6},{5,7},{6,4},{7,5},{8,10},{9,11},{10,... | collective-permute-start | bytes 393224 | tf_op jit(solution)/shard_map/ppermute | solution.py:508
  50.9 1.4 %collective-permute-done.9 = f32[2,128,128]{2,1,0:T(8,128)S(1)} collective-permute-done((f32[2,128,128]{2,1,0:T(8,128)S(1)}, f32[2,128,128]{2,1,0:T(8,128)S(1)}, u32[]{:S(2)}, u32[]{:S(2)}) %collective-permute-start.9) | collective-permute-done | bytes 131104 | tf_op jit(solution)/shard_map/ppermute | solution.py:508
  52.3 2.5 %collective-permute-done.8 = f32[2,128,128]{2,1,0:T(8,128)S(1)} collective-permute-done((f32[2,128,128]{2,1,0:T(8,128)S(1)}, f32[2,128,128]{2,1,0:T(8,128)S(1)}, u32[]{:S(2)}, u32[]{:S(2)}) %collective-permute-start.8) | collective-permute-done | bytes 131104 | tf_op jit(solution)/shard_map/ppermute | solution.py:508
  54.9 1.6 %collective-permute-start.13 = (f32[4,128,128]{2,1,0:T(8,128)S(1)}, f32[4,128,128]{2,1,0:T(8,128)S(1)}, u32[]{:S(2)}, u32[]{:S(2)}) collective-permute-start(f32[4,128,128]{2,1,0:T(8,128)S(1)} %pad_maximum_fusion.4.same_ref), channel_id=1, source_target_pairs={{0,1},{1,0},{2,3},{3,2},{4,5},{5,4},{6,7},{7,6},{8,9},{9,8},{10,11... | collective-permute-start | bytes 786440 | tf_op jit(solution)/shard_map/ppermute | solution.py:511
  56.4 0.0 collective-permute-done.4
  56.5 0.0 collective-permute-done.3
  56.5 0.0 collective-permute-done.2
  56.5 0.6 collective-permute-start.12
  57.2 6.9 %collective-permute-done.13.cross_ref = f32[4,128,128]{2,1,0:T(8,128)S(1)} collective-permute-done((f32[4,128,128]{2,1,0:T(8,128)S(1)}, f32[4,128,128]{2,1,0:T(8,128)S(1)}, u32[]{:S(2)}, u32[]{:S(2)}) %collective-permute-start.13) | collective-permute-done | bytes 262176 | tf_op jit(solution)/shard_map/ppermute | solution.py:511
  64.2 1.1 %collective-permute-start.15 = (f32[2,4,128,128]{3,2,1,0:T(8,128)S(1)}, f32[2,4,128,128]{3,2,1,0:T(8,128)S(1)}, u32[]{:S(2)}, u32[]{:S(2)}) collective-permute-start(f32[2,4,128,128]{3,2,1,0:T(8,128)S(1)} %pad_maximum_fusion.1), channel_id=1, source_target_pairs={{0,2},{1,7},{2,4},{3,1},{4,6},{5,3},{6,0},{7,5},{8,10},{9,15},{10,... | collective-permute-start | bytes 1572872 | tf_op jit(solution)/shard_map/ppermute | solution.py:513
  65.3 0.5 collective-permute-start.11
  65.8 3.9 %collective-permute-done.12.cross_ref = f32[4,128,128]{2,1,0:T(8,128)S(1)} collective-permute-done((f32[4,128,128]{2,1,0:T(8,128)S(1)}, f32[4,128,128]{2,1,0:T(8,128)S(1)}, u32[]{:S(2)}, u32[]{:S(2)}) %collective-permute-start.12) | collective-permute-done | bytes 262176 | tf_op jit(solution)/shard_map/ppermute | solution.py:511
  69.7 0.0 copy-start.6
  69.8 0.5 collective-permute-start.14
  70.3 1.2 %collective-permute-start.5 = (f32[4,128,128]{2,1,0:T(8,128)S(1)}, f32[4,128,128]{2,1,0:T(8,128)S(1)}, u32[]{:S(2)}, u32[]{:S(2)}) collective-permute-start(f32[4,128,128]{2,1,0:T(8,128)S(1)} %get-tuple-element.44.same_ref), channel_id=1, source_target_pairs={{0,1},{1,0},{2,3},{3,2},{4,5},{5,4},{6,7},{7,6},{8,9},{9,8},{10,11... | collective-permute-start | bytes 786440 | tf_op jit(solution)/shard_map/ppermute | solution.py:512
  71.4 0.0 copy-done.1
  71.4 0.0 copy-done.4
  71.4 0.7 rows_step.7.refs_0_
  72.1 3.2 %collective-permute-done.11.cross_ref = f32[4,128,128]{2,1,0:T(8,128)S(1)} collective-permute-done((f32[4,128,128]{2,1,0:T(8,128)S(1)}, f32[4,128,128]{2,1,0:T(8,128)S(1)}, u32[]{:S(2)}, u32[]{:S(2)}) %collective-permute-start.11) | collective-permute-done | bytes 262176 | tf_op jit(solution)/shard_map/ppermute | solution.py:512
  75.4 0.7 rows_step.5.refs_0_
  76.1 0.0 copy-done
  76.1 0.0 copy-done.3
  76.1 0.7 rows_step.8.near_ref
  76.9 2.9 %collective-permute-done.5.cross_ref = f32[4,128,128]{2,1,0:T(8,128)S(1)} collective-permute-done((f32[4,128,128]{2,1,0:T(8,128)S(1)}, f32[4,128,128]{2,1,0:T(8,128)S(1)}, u32[]{:S(2)}, u32[]{:S(2)}) %collective-permute-start.5) | collective-permute-done | bytes 262176 | tf_op jit(solution)/shard_map/ppermute | solution.py:512
  79.7 0.7 rows_step.6.own_ref
  80.5 0.3 collective-permute-done.15
  80.9 0.7 rows_step.9.refs_0_
  81.6 7.1 %collective-permute-done.14 = f32[2,4,128,128]{3,2,1,0:T(8,128)S(1)} collective-permute-done((f32[2,4,128,128]{3,2,1,0:T(8,128)S(1)}, f32[2,4,128,128]{3,2,1,0:T(8,128)S(1)}, u32[]{:S(2)}, u32[]{:S(2)}) %collective-permute-start.14) | collective-permute-done | bytes 524320 | tf_op jit(solution)/shard_map/ppermute | solution.py:513
  88.7 0.0 copy-done.6
  88.7 5.8 %focus_step.1 = f32[2,1,1024,128]{3,2,1,0:T(8,128)} custom-call(s32[1]{0:T(128)} %bitcast.place_ref.origin_ref, s32[1]{0:T(128)S(6)} %select_n.17.origin_ref, s32[1,2]{1,0:T(1,128)S(1)} %copy-done.6, bf16[768,512]{1,0:T(8,128)(2,1)S(1)} %copy-done, f32[8,256]{1,0:T(8,128)S(1)} %copy-done.3, f32[4,2,128,256]{3,2,1,0:T(8,128)S(1)} %rows_step.6.own_ref, ...), custom_call_target="tpu_custom_call" | custom-call | flops 480000000 | tf_op jit(solution)/shard_map/focus_step/pallas_call | solution.py:459
  (16 shorter events, 0.3 us)
Async XLA Ops:
  3.8 4.6 %copy-start.7 = (f32[2,64,1024]{2,1,0:T(8,128)S(1)}, f32[2,64,1024]{2,1,0:T(8,128)}, u32[]{:S(2)}) copy-start(f32[2,64,1024]{2,1,0:T(8,128)} %get-tuple-element.19) | copy-start | bytes 1572868
  3.8 4.6 %copy-start.8 = (f32[2,64,1024]{2,1,0:T(8,128)S(1)}, f32[2,64,1024]{2,1,0:T(8,128)}, u32[]{:S(2)}) copy-start(f32[2,64,1024]{2,1,0:T(8,128)} %get-tuple-element.21) | copy-start | bytes 1572868
  3.8 21.5 %copy-start.2 = (bf16[256,1536]{1,0:T(8,128)(2,1)S(1)}, bf16[256,1536]{1,0:T(8,128)(2,1)}, u32[]{:S(2)}) copy-start(bf16[256,1536]{1,0:T(8,128)(2,1)} %constant.58.clone.table_ref) | copy-start | bytes 2359300
  3.8 21.5 %copy-start.5 = (f32[8,256]{1,0:T(8,128)S(1)}, f32[8,256]{1,0:T(8,128)}, u32[]{:S(2)}) copy-start(f32[8,256]{1,0:T(8,128)} %constant.59.clone.turn_ref) | copy-start | bytes 24580
  3.8 4.6 %collective-permute-start = (f32[2,2,64,1024]{3,2,1,0:T(8,128)}, f32[2,2,64,1024]{3,2,1,0:T(8,128)S(1)}, u32[]{:S(2)}, u32[]{:S(2)}) collective-permute-start(f32[2,2,64,1024]{3,2,1,0:T(8,128)} %get-tuple-element.20), channel_id=1, source_target_pairs={{0,8},{8,0},{16,24},{24,16},{1,9},{9,1},{17,25},{25,17},{2,10},{10... | collective-permute-start | bytes 3145736 | tf_op jit(solution)/shard_map/ppermute | solution.py:499
  8.3 4.0 %collective-permute-start.6 = (f32[2,2,64,1024]{3,2,1,0:T(8,128)}, f32[2,2,64,1024]{3,2,1,0:T(8,128)S(1)}, u32[]{:S(2)}, u32[]{:S(2)}) collective-permute-start(f32[2,2,64,1024]{3,2,1,0:T(8,128)} %get-tuple-element.27), channel_id=1, source_target_pairs={{0,8},{8,0},{16,24},{24,16},{1,9},{9,1},{17,25},{25,17},{2,10},{10... | collective-permute-start | bytes 3145736 | tf_op jit(solution)/shard_map/ppermute | solution.py:499
  8.4 63.0 %copy-start.1 = (bf16[768,512]{1,0:T(8,128)(2,1)S(1)}, bf16[768,512]{1,0:T(8,128)(2,1)}, u32[]{:S(2)}) copy-start(bf16[768,512]{1,0:T(8,128)(2,1)} %constant.66.table_ref) | copy-start | bytes 2359300
  8.4 63.0 %copy-start.4 = (f32[8,256]{1,0:T(8,128)S(1)}, f32[8,256]{1,0:T(8,128)}, u32[]{:S(2)}) copy-start(f32[8,256]{1,0:T(8,128)} %constant.61.clone.turn_ref) | copy-start | bytes 24580
  9.4 16.0 %collective-permute-start.1 = (f32[2,64,1024]{2,1,0:T(8,128)}, f32[2,64,1024]{2,1,0:T(8,128)}, u32[]{:S(2)}, u32[]{:S(2)}) collective-permute-start(f32[2,64,1024]{2,1,0:T(8,128)} %get-tuple-element.35), channel_id=1, source_target_pairs={{0,16},{8,24},{16,0},{24,8},{1,17},{9,25},{17,1},{25,9},{2,18},{10... | collective-permute-start | bytes 1572872 | tf_op jit(solution)/shard_map/ppermute | solution.py:502
  14.4 61.7 %copy-start = (bf16[768,512]{1,0:T(8,128)(2,1)S(1)}, bf16[768,512]{1,0:T(8,128)(2,1)}, u32[]{:S(2)}) copy-start(bf16[768,512]{1,0:T(8,128)(2,1)} %constant.65.table_ref) | copy-start | bytes 2359300
  14.4 61.7 %copy-start.3 = (f32[8,256]{1,0:T(8,128)S(1)}, f32[8,256]{1,0:T(8,128)}, u32[]{:S(2)}) copy-start(f32[8,256]{1,0:T(8,128)} %constant.63.clone.turn_ref) | copy-start | bytes 24580
  14.4 21.7 %collective-permute-start.7 = (f32[2,64,1024]{2,1,0:T(8,128)}, f32[2,64,1024]{2,1,0:T(8,128)}, u32[]{:S(2)}, u32[]{:S(2)}) collective-permute-start(f32[2,64,1024]{2,1,0:T(8,128)} %get-tuple-element.33), channel_id=1, source_target_pairs={{0,16},{8,24},{16,0},{24,8},{1,17},{9,25},{17,1},{25,9},{2,18},{10... | collective-permute-start | bytes 1572872 | tf_op jit(solution)/shard_map/ppermute | solution.py:502
  27.1 29.3 %collective-permute-start.4 = (f32[2,128,128]{2,1,0:T(8,128)S(1)}, f32[2,128,128]{2,1,0:T(8,128)S(1)}, u32[]{:S(2)}, u32[]{:S(2)}) collective-permute-start(f32[2,128,128]{2,1,0:T(8,128)S(1)} %get-tuple-element.25), channel_id=1, source_target_pairs={{0,6},{1,7},{2,4},{3,5},{4,2},{5,3},{6,0},{7,1},{8,14},{9,15},{10,... | collective-permute-start | bytes 393224 | tf_op jit(solution)/shard_map/ppermute | solution.py:508
  31.3 25.2 %collective-permute-start.3 = (f32[2,128,128]{2,1,0:T(8,128)S(1)}, f32[2,128,128]{2,1,0:T(8,128)S(1)}, u32[]{:S(2)}, u32[]{:S(2)}) collective-permute-start(f32[2,128,128]{2,1,0:T(8,128)S(1)} %get-tuple-element.24), channel_id=1, source_target_pairs={{0,4},{1,5},{2,6},{3,7},{4,0},{5,1},{6,2},{7,3},{8,12},{9,13},{10,... | collective-permute-start | bytes 393224 | tf_op jit(solution)/shard_map/ppermute | solution.py:508
  31.3 25.2 %collective-permute-start.2 = (f32[2,128,128]{2,1,0:T(8,128)S(1)}, f32[2,128,128]{2,1,0:T(8,128)S(1)}, u32[]{:S(2)}, u32[]{:S(2)}) collective-permute-start(f32[2,128,128]{2,1,0:T(8,128)S(1)} %get-tuple-element.23), channel_id=1, source_target_pairs={{0,2},{1,3},{2,0},{3,1},{4,6},{5,7},{6,4},{7,5},{8,10},{9,11},{10,... | collective-permute-start | bytes 393224 | tf_op jit(solution)/shard_map/ppermute | solution.py:508
  37.8 8.3 %collective-permute-start.10 = (f32[2,128,128]{2,1,0:T(8,128)S(1)}, f32[2,128,128]{2,1,0:T(8,128)S(1)}, u32[]{:S(2)}, u32[]{:S(2)}) collective-permute-start(f32[2,128,128]{2,1,0:T(8,128)S(1)} %get-tuple-element.32), channel_id=1, source_target_pairs={{0,6},{1,7},{2,4},{3,5},{4,2},{5,3},{6,0},{7,1},{8,14},{9,15},{10,... | collective-permute-start | bytes 393224 | tf_op jit(solution)/shard_map/ppermute | solution.py:508
  41.7 10.6 %collective-permute-start.9 = (f32[2,128,128]{2,1,0:T(8,128)S(1)}, f32[2,128,128]{2,1,0:T(8,128)S(1)}, u32[]{:S(2)}, u32[]{:S(2)}) collective-permute-start(f32[2,128,128]{2,1,0:T(8,128)S(1)} %get-tuple-element.31), channel_id=1, source_target_pairs={{0,4},{1,5},{2,6},{3,7},{4,0},{5,1},{6,2},{7,3},{8,12},{9,13},{10,... | collective-permute-start | bytes 393224 | tf_op jit(solution)/shard_map/ppermute | solution.py:508
  46.1 8.8 %collective-permute-start.8 = (f32[2,128,128]{2,1,0:T(8,128)S(1)}, f32[2,128,128]{2,1,0:T(8,128)S(1)}, u32[]{:S(2)}, u32[]{:S(2)}) collective-permute-start(f32[2,128,128]{2,1,0:T(8,128)S(1)} %get-tuple-element.30), channel_id=1, source_target_pairs={{0,2},{1,3},{2,0},{3,1},{4,6},{5,7},{6,4},{7,5},{8,10},{9,11},{10,... | collective-permute-start | bytes 393224 | tf_op jit(solution)/shard_map/ppermute | solution.py:508
  54.9 9.2 %collective-permute-start.13 = (f32[4,128,128]{2,1,0:T(8,128)S(1)}, f32[4,128,128]{2,1,0:T(8,128)S(1)}, u32[]{:S(2)}, u32[]{:S(2)}) collective-permute-start(f32[4,128,128]{2,1,0:T(8,128)S(1)} %pad_maximum_fusion.4.same_ref), channel_id=1, source_target_pairs={{0,1},{1,0},{2,3},{3,2},{4,5},{5,4},{6,7},{7,6},{8,9},{9,8},{10,11... | collective-permute-start | bytes 786440 | tf_op jit(solution)/shard_map/ppermute | solution.py:511
  56.5 13.2 %collective-permute-start.12 = (f32[4,128,128]{2,1,0:T(8,128)S(1)}, f32[4,128,128]{2,1,0:T(8,128)S(1)}, u32[]{:S(2)}, u32[]{:S(2)}) collective-permute-start(f32[4,128,128]{2,1,0:T(8,128)S(1)} %pad_maximum_fusion.2.same_ref), channel_id=1, source_target_pairs={{0,1},{1,0},{2,3},{3,2},{4,5},{5,4},{6,7},{7,6},{8,9},{9,8},{10,11... | collective-permute-start | bytes 786440 | tf_op jit(solution)/shard_map/ppermute | solution.py:511
  64.2 16.6 %collective-permute-start.15 = (f32[2,4,128,128]{3,2,1,0:T(8,128)S(1)}, f32[2,4,128,128]{3,2,1,0:T(8,128)S(1)}, u32[]{:S(2)}, u32[]{:S(2)}) collective-permute-start(f32[2,4,128,128]{3,2,1,0:T(8,128)S(1)} %pad_maximum_fusion.1), channel_id=1, source_target_pairs={{0,2},{1,7},{2,4},{3,1},{4,6},{5,3},{6,0},{7,5},{8,10},{9,15},{10,... | collective-permute-start | bytes 1572872 | tf_op jit(solution)/shard_map/ppermute | solution.py:513
  65.3 10.1 %collective-permute-start.11 = (f32[4,128,128]{2,1,0:T(8,128)S(1)}, f32[4,128,128]{2,1,0:T(8,128)S(1)}, u32[]{:S(2)}, u32[]{:S(2)}) collective-permute-start(f32[4,128,128]{2,1,0:T(8,128)S(1)} %get-tuple-element.42.same_ref), channel_id=1, source_target_pairs={{0,1},{1,0},{2,3},{3,2},{4,5},{5,4},{6,7},{7,6},{8,9},{9,8},{10,11... | collective-permute-start | bytes 786440 | tf_op jit(solution)/shard_map/ppermute | solution.py:512
  69.7 19.0 %copy-start.6 = (s32[1,2]{1,0:T(1,128)S(1)}, s32[1,2]{1,0:T(1,128)}, u32[]{:S(2)}) copy-start(s32[1,2]{1,0:T(1,128)} %widths_ref.1) | copy-start | bytes 28
  69.8 18.9 %collective-permute-start.14 = (f32[2,4,128,128]{3,2,1,0:T(8,128)S(1)}, f32[2,4,128,128]{3,2,1,0:T(8,128)S(1)}, u32[]{:S(2)}, u32[]{:S(2)}) collective-permute-start(f32[2,4,128,128]{3,2,1,0:T(8,128)S(1)} %pad_maximum_fusion), channel_id=1, source_target_pairs={{0,2},{1,7},{2,4},{3,1},{4,6},{5,3},{6,0},{7,5},{8,10},{9,15},{10,... | collective-permute-start | bytes 1572872 | tf_op jit(solution)/shard_map/ppermute | solution.py:513
  70.3 9.5 %collective-permute-start.5 = (f32[4,128,128]{2,1,0:T(8,128)S(1)}, f32[4,128,128]{2,1,0:T(8,128)S(1)}, u32[]{:S(2)}, u32[]{:S(2)}) collective-permute-start(f32[4,128,128]{2,1,0:T(8,128)S(1)} %get-tuple-element.44.same_ref), channel_id=1, source_target_pairs={{0,1},{1,0},{2,3},{3,2},{4,5},{5,4},{6,7},{7,6},{8,9},{9,8},{10,11... | collective-permute-start | bytes 786440 | tf_op jit(solution)/shard_map/ppermute | solution.py:512
